TPU v7x, 256 devices: a 8x8x2 block of a 8x8x16 slice. The times are simulated.
256 devices in a mesh: rep: 2 (over z), gx: 128 (over y, x, core).
Axes of the slice: x: 8, y: 8, z: 2, core: 2. Of those that a mesh axis runs over, the one named last changes fastest.
The devices are a block of a 8x8x16 slice.
Arguments:
- positions: float32 [3, 1048576], P(None, ('rep', 'gx')), parts along dimension 1, may hold values from 0 to 512, as said below
- polar: float32 [1048576], P(('rep', 'gx')), parts along dimension 0, may hold values from 0.25 to 1
- field_ext: float32 [3, 1048576], P(None, ('rep', 'gx')), parts along dimension 1, may hold values from -10 to 10
- tile_atom: int32 [1048576], P(('rep', 'gx')), parts along dimension 0, may hold values from 0 to 4095, as said below
- tile_list: int32 [8192, 3], P(('rep', 'gx')), parts along dimension 0, may hold values from 0 to 63, as said below
- image_shift: int32 [2, 8192, 3], P(None, ('rep', 'gx')), parts along dimension 1, may hold values from 0 to 1, as said below
Outputs:
- dipoles: float32 [3, 1048576], P(None, ('rep', 'gx')), parts along dimension 1
- residual: float32 [3, 1048576], P(None, ('rep', 'gx')), parts along dimension 1
There are 2 independent parts, one for each index of `rep`. A program takes and returns all parts, laid end to end along the dimension named above; each array names one. Nothing has to cross between parts.
Inputs may be any that keep to these rules, and one draw needn't show every extreme that they name: `positions`: coordinates lie in a box of 512 by 128 by 64; the atoms of slab s have first coordinate between 4 s and 4 s + 4; no two atoms, and no atom and a periodic image of another, are closer than 1.4. `tile_atom`: for each slab, a permutation of 0 to 4095. `tile_list`: entry 0 of a tile is the tile's own index within its slab. Entry n of a tile of slab s names tile n of slab s if n < 32, else tile n - 32 of slab s + 1 (slab 0 after the last). `image_shift`: offsets along the second and third coordinates in box lengths, one pair for each entry of tile_list; zero for entry 0.
All inputs are finite; a program needn't handle non-finite values.
Results may differ from a plain program's by a relative error of at most 0.0003.
Values sent between devices are 32-bit elements; how exact they have to be, the bound alone decides.
No kernel may reach another device: no remote copies, remote signals or barrier semaphores. Data moves between devices by JAX's collectives and lax.ppermute only.
A program may use at most 64 MiB of HBM per device.

v0:
```python
import functools
import math

import jax
import jax.numpy as jnp
from jax import lax
from jax.sharding import Mesh
from jax.sharding import PartitionSpec as P

ITERS = 4
GX = ("gx_0", "gx_1", "gx_2")
REP_GX = ("rep", "gx_0", "gx_1", "gx_2")


thole_factor = 0.39


def over_axes(shard, axes):
    return functools.reduce(lax.psum, axes, shard)


def passed_along(value, axis, steps):
    count = lax.axis_size(axis)
    pairs = [(source, (source + steps) % count) for source in range(count)]
    return lax.ppermute(value, axis, pairs)


def pair_block(
    place_left, root_left, moment_left, place_right, root_right, moment_right, weights, self_flags
):
    offset_x = place_right[:, 0, None, :] - place_left[:, 0, :, None]
    offset_y = place_right[:, 1, None, :] - place_left[:, 1, :, None]
    offset_z = place_right[:, 2, None, :] - place_left[:, 2, :, None]
    dist_sq = offset_x * offset_x + offset_y * offset_y + offset_z * offset_z
    tile_width = place_left.shape[2]
    row_ids = lax.broadcasted_iota(jnp.int32, (tile_width, tile_width), 0)
    column_ids = lax.broadcasted_iota(jnp.int32, (tile_width, tile_width), 1)
    same_atom = jnp.logical_and(self_flags[:, None, None] > 0, (row_ids == column_ids)[None])
    dist_sq = jnp.where(same_atom, 1.0, dist_sq)
    inv_dist = lax.rsqrt(dist_sq)
    distance = dist_sq * inv_dist
    damp_arg = thole_factor * dist_sq * distance / (root_left[:, :, None] * root_right[:, None, :])
    decay = jnp.exp(-damp_arg)
    inv_cube = jnp.where(same_atom, 0.0, weights[:, None, None] * inv_dist * inv_dist * inv_dist)
    coeff_three = (1.0 - decay) * inv_cube
    coeff_five = 3.0 * (1.0 - (1.0 + damp_arg) * decay) * inv_cube * inv_dist * inv_dist
    offsets = (offset_x, offset_y, offset_z)
    proj_right = (
        offset_x * moment_right[:, 0, None, :]
        + offset_y * moment_right[:, 1, None, :]
        + offset_z * moment_right[:, 2, None, :]
    )
    proj_left = (
        offset_x * moment_left[:, 0, :, None]
        + offset_y * moment_left[:, 1, :, None]
        + offset_z * moment_left[:, 2, :, None]
    )
    lift_right = coeff_five * proj_right
    lift_left = coeff_five * proj_left
    field_left = jnp.stack(
        [
            jnp.sum(
                lift_right * offsets[component] - coeff_three * moment_right[:, component, None, :],
                axis=2,
            )
            for component in range(3)
        ],
        axis=1,
    )
    field_right = jnp.stack(
        [
            jnp.sum(
                lift_left * offsets[component] - coeff_three * moment_left[:, component, :, None],
                axis=1,
            )
            for component in range(3)
        ],
        axis=1,
    )
    return (field_left, field_right)


def slab_fields(
    window_place,
    window_root,
    window_moment,
    left_index,
    right_index,
    image_vec,
    weights,
    self_flags,
):
    entries = left_index.shape[0]
    block_size = math.gcd(entries, 32)
    window_size = window_place.shape[0]
    tile_width = window_place.shape[2]
    slot_ids = jnp.arange(window_size, dtype=jnp.int32)

    def accumulate(summed, first_entry):
        left_rows = lax.dynamic_slice_in_dim(left_index, first_entry, block_size)
        right_rows = lax.dynamic_slice_in_dim(right_index, first_entry, block_size)
        image_rows = lax.dynamic_slice_in_dim(image_vec, first_entry, block_size)
        weight_rows = lax.dynamic_slice_in_dim(weights, first_entry, block_size)
        flag_rows = lax.dynamic_slice_in_dim(self_flags, first_entry, block_size)
        place_left = jnp.take(window_place, left_rows, axis=0)
        place_right = jnp.take(window_place, right_rows, axis=0) + image_rows[:, :, None]
        field_left, field_right = pair_block(
            place_left,
            jnp.take(window_root, left_rows, axis=0),
            jnp.take(window_moment, left_rows, axis=0),
            place_right,
            jnp.take(window_root, right_rows, axis=0),
            jnp.take(window_moment, right_rows, axis=0),
            weight_rows,
            flag_rows,
        )
        hit_left = (left_rows[:, None] == slot_ids[None, :]).astype(jnp.float32)
        hit_right = (right_rows[:, None] == slot_ids[None, :]).astype(jnp.float32)
        summed = summed + jnp.einsum(
            "ew,ef->wf",
            hit_left,
            field_left.reshape(block_size, 3 * tile_width),
            precision=lax.Precision.HIGHEST,
        )
        summed = summed + jnp.einsum(
            "ew,ef->wf",
            hit_right,
            field_right.reshape(block_size, 3 * tile_width),
            precision=lax.Precision.HIGHEST,
        )
        return (summed, None)

    first_entries = jnp.arange(0, entries, block_size, dtype=jnp.int32)
    summed, _ = lax.scan(
        accumulate, jnp.zeros((window_size, 3 * tile_width), jnp.float32), first_entries
    )
    return summed.reshape(window_size, 3, tile_width)


def image_vectors(lists, shifts, last_flag, tile_count, box_x, box_y, box_z):
    crossing = lists >= tile_count
    wrapped = jnp.where(jnp.logical_and(crossing, last_flag), box_x, 0.0)
    vectors = jnp.stack(
        [wrapped, shifts[0].astype(jnp.float32) * box_y, shifts[1].astype(jnp.float32) * box_z],
        axis=-1,
    )
    return vectors.reshape(-1, 3)


def two_products(vector, applied):
    return (over_axes(jnp.sum(vector * vector), GX), over_axes(jnp.sum(vector * applied), GX))


def on_device(positions, polar, field_ext, tile_atom, tile_list, image_shift):
    tile_count = tile_list.shape[0]
    links = tile_list.shape[1]
    atom_count = tile_atom.shape[0]
    tile_width = atom_count // tile_count
    slab_count = lax.axis_size(GX)
    position_id = lax.axis_index(GX)
    tiled_place = positions[:, tile_atom].reshape(3, tile_count, tile_width).transpose(1, 0, 2)
    tiled_polar = polar[tile_atom].reshape(tile_count, tile_width)
    tiled_root = jnp.sqrt(tiled_polar)
    tiled_rhs = field_ext[:, tile_atom].reshape(3, tile_count, tile_width).transpose(1, 0, 2)
    packed = jnp.concatenate([tiled_place, tiled_root[:, None, :]], axis=1)
    box_x = 4.0 * slab_count
    box_y = 128.0
    box_z = 2.0 * tile_count
    entry_ids = jnp.arange(links, dtype=jnp.int32)
    own_left = jnp.repeat(jnp.arange(tile_count, dtype=jnp.int32), links)
    own_right = tile_list.reshape(-1)
    own_weights = jnp.tile(jnp.where(entry_ids == 0, 0.5, 1.0), tile_count)
    own_self = jnp.tile((entry_ids == 0).astype(jnp.int32), tile_count)
    own_image = image_vectors(
        tile_list, image_shift, position_id == slab_count - 1, tile_count, box_x, box_y, box_z
    )
    ahead = passed_along(packed, GX, -1)
    window_pack = jnp.concatenate([packed, ahead], axis=0)

    def operate(direction):
        ahead_moment = passed_along(direction, GX, -1)
        summed = slab_fields(
            window_pack[:, :3],
            window_pack[:, 3],
            jnp.concatenate([direction, ahead_moment], axis=0),
            own_left,
            own_right,
            own_image,
            own_weights,
            own_self,
        )
        returned = passed_along(summed[tile_count:], GX, 1)
        return direction / tiled_polar[:, None, :] - (summed[:tile_count] + returned)

    solution = jnp.zeros_like(tiled_rhs)
    resid = tiled_rhs
    applied = operate(resid)
    norm_now, product = two_products(resid, applied)
    step_size = norm_now / product
    direction, along = (resid, applied)
    for iteration in range(ITERS):
        solution = solution + step_size * direction
        resid = resid - step_size * along
        if iteration + 1 < ITERS:
            applied = operate(resid)
            norm_next, product = two_products(resid, applied)
            ratio = norm_next / norm_now
            step_size = norm_next / (product - ratio * norm_next / step_size)
            direction = resid + ratio * direction
            along = applied + ratio * along
            norm_now = norm_next
    dipoles = (
        jnp.zeros((3, atom_count), jnp.float32)
        .at[:, tile_atom]
        .set(solution.transpose(1, 0, 2).reshape(3, atom_count))
    )
    residual = (
        jnp.zeros((3, atom_count), jnp.float32)
        .at[:, tile_atom]
        .set(resid.transpose(1, 0, 2).reshape(3, atom_count))
    )
    return (dipoles, residual)


def solution(mesh):
    split = Mesh(mesh.devices.reshape(mesh.shape["rep"], 8, 8, 2), ("rep", "gx_0", "gx_1", "gx_2"))
    return jax.shard_map(
        on_device,
        mesh=split,
        in_specs=(
            P(None, REP_GX),
            P(REP_GX),
            P(None, REP_GX),
            P(REP_GX),
            P(REP_GX, None),
            P(None, REP_GX, None),
        ),
        out_specs=(P(None, REP_GX), P(None, REP_GX)),
        check_vma=False,
    )
```

profile of v0, /device:TPU:513, one launch (start us, length us, event | category | flops | bytes accessed | tf_op | source)
XLA Modules:
  0.0 492.2 jit_solution(17890280772441615265)
XLA Ops:
  1.4 23.0 %gather_fusion.25 = f32[4096]{0:T(1024)S(1)} fusion(f32[4096]{0:T(1024)S(1)} %copy-done, s32[4096]{0:T(1024)S(1)} %get-tuple-element.975), kind=kCustom, calls=%fused_computation.25 | custom fusion | bytes 49152 | tf_op jit(solution)/shard_map/gather | solution.py:162
  25.1 14.1 %gather_fusion.26 = f32[4096,3]{1,0:T(8,128)} fusion(f32[3,4096]{0,1:T(8,128)S(1)} %copy.89, s32[4096]{0:T(1024)S(1)} %get-tuple-element.975), kind=kCustom, calls=%fused_computation.26 | custom fusion | bytes 114688 | tf_op jit(solution)/shard_map/gather | solution.py:161
  39.2 2.2 copy.90
  41.4 20.5 %collective-permute-start = (f32[32,4,128]{2,0,1:T(8,128)S(1)}, f32[32,4,128]{2,0,1:T(8,128)S(1)}, u32[]{:S(2)}, u32[]{:S(2)}) collective-permute-start(f32[32,4,128]{2,0,1:T(8,128)S(1)} %pad_maximum_fusion.5), channel_id=1, source_target_pairs={{0,127},{1,0},{2,1},{3,2},{4,3},{5,4},{6,5},{7,6},{8,7},{9,8},{10,... | collective-permute-start | bytes 196616 | tf_op jit(solution)/shard_map/ppermute | solution.py:25
  62.6 14.1 %gather_fusion.24 = f32[4096,3]{1,0:T(8,128)} fusion(f32[3,4096]{0,1:T(8,128)S(1)} %copy.86, s32[4096]{0:T(1024)S(1)} %get-tuple-element.975), kind=kCustom, calls=%fused_computation.24 | custom fusion | bytes 114688 | tf_op jit(solution)/shard_map/gather | solution.py:164
  76.7 2.2 copy.87
  80.3 2.4 collective-permute-done.1
  82.9 46.8 %while.48 = (s32[]{:T(128)}, f32[64,384]{1,0:T(8,128)S(1)}, s32[3]{0:T(128)S(1)}, s32[96]{0:T(128)S(1)}, s32[96]{0:T(128)S(1)}, /*index=5*/s32[96]{0:T(128)S(1)}...) while((s32[]{:T(128)}, f32[64,384]{1,0:T(8,128)S(1)}, ...), condition=%wide.region_11.14_spmd.clone.clone, body=%wide.region_4.13_spmd.clone.clone.sunk | while | flops 53144164 | bytes 2176077 | solution.py:134
  90.0 7.8 %fusion.181 = (f32[32,128]{1,0:T(8,128)S(1)}, f32[32,128]{1,0:T(8,128)S(1)}, f32[32,128]{1,0:T(8,128)S(1)}, f32[32,128]{1,0:T(8,128)S(1)}, f32[32,128]{1,0:T(8,128)S(1)}, /*index=5*/f32[32,128]{1,0:T(8,128)S(1)}) fusion(f32[32,128]{1,0:T(8,128)S(1)} %bitcast.385, f32[32,128]{1,0:T(8,128)S(1)} %bitcast.397, f32[32,128]{1,0:T(8,128)S(1)} %bitcast.361, ...), kind=kLoop, calls=%fused_computation.66.clone.1 | loop fusion | flops 34054144 | bytes 344224 | tf_op jit(solution)/shard_map/while/body/eval_jaxpr/reduce_sum | solution.py:72
  105.6 7.8 %fusion.181 = (f32[32,128]{1,0:T(8,128)S(1)}, f32[32,128]{1,0:T(8,128)S(1)}, f32[32,128]{1,0:T(8,128)S(1)}, f32[32,128]{1,0:T(8,128)S(1)}, f32[32,128]{1,0:T(8,128)S(1)}, /*index=5*/f32[32,128]{1,0:T(8,128)S(1)}) fusion(f32[32,128]{1,0:T(8,128)S(1)} %bitcast.385, f32[32,128]{1,0:T(8,128)S(1)} %bitcast.397, f32[32,128]{1,0:T(8,128)S(1)} %bitcast.361, ...), kind=kLoop, calls=%fused_computation.66.clone.1 | loop fusion | flops 34054144 | bytes 344224 | tf_op jit(solution)/shard_map/while/body/eval_jaxpr/reduce_sum | solution.py:72
  121.2 7.8 %fusion.181 = (f32[32,128]{1,0:T(8,128)S(1)}, f32[32,128]{1,0:T(8,128)S(1)}, f32[32,128]{1,0:T(8,128)S(1)}, f32[32,128]{1,0:T(8,128)S(1)}, f32[32,128]{1,0:T(8,128)S(1)}, /*index=5*/f32[32,128]{1,0:T(8,128)S(1)}) fusion(f32[32,128]{1,0:T(8,128)S(1)} %bitcast.385, f32[32,128]{1,0:T(8,128)S(1)} %bitcast.397, f32[32,128]{1,0:T(8,128)S(1)} %bitcast.361, ...), kind=kLoop, calls=%fused_computation.66.clone.1 | loop fusion | flops 34054144 | bytes 344224 | tf_op jit(solution)/shard_map/while/body/eval_jaxpr/reduce_sum | solution.py:72
  129.9 1.3 collective-permute-done.2
  131.9 11.4 %all-reduce.7 = (f32[]{:T(128)}, f32[]{:T(128)}) all-reduce(f32[]{:T(128)} %get-tuple-element.759, f32[]{:T(128)} %get-tuple-element.758), channel_id=1, replica_groups=mesh['rep'=2,'gx_0'=8,'gx_1'=8,'gx_2'=2] {'gx_0'}, use_global_device_ids=true, to_apply=%region_1.2 | all-reduce | flops 2 | bytes 16 | tf_op jit(solution)/shard_map/psum | solution.py:19
  143.2 14.6 %all-reduce.3 = (f32[]{:T(128)}, f32[]{:T(128)}) all-reduce(f32[]{:T(128)} %get-tuple-element.862, f32[]{:T(128)} %get-tuple-element.863), channel_id=1, replica_groups=mesh['rep'=2,'gx_0'=8,'gx_1'=8,'gx_2'=2] {'gx_1'}, use_global_device_ids=true, to_apply=%region_2.3 | all-reduce | flops 2 | bytes 16 | tf_op jit(solution)/shard_map/psum | solution.py:19
  157.9 10.4 %all-reduce.11 = (f32[]{:T(128)}, f32[]{:T(128)}) all-reduce(f32[]{:T(128)} %get-tuple-element.854, f32[]{:T(128)} %get-tuple-element.855), channel_id=1, replica_groups=mesh['rep'=2,'gx_0'=8,'gx_1'=8,'gx_2'=2] {'gx_2'}, use_global_device_ids=true, to_apply=%region_3.4 | all-reduce | flops 2 | bytes 16 | tf_op jit(solution)/shard_map/psum | solution.py:19
  170.1 3.5 collective-permute-done.3
  173.7 47.5 %while.49 = (s32[]{:T(128)}, f32[64,384]{1,0:T(8,128)S(1)}, s32[3]{0:T(128)S(1)}, s32[96]{0:T(128)S(1)}, s32[96]{0:T(128)S(1)}, /*index=5*/s32[96]{0:T(128)S(1)}...) while((s32[]{:T(128)}, f32[64,384]{1,0:T(8,128)S(1)}, ...), condition=%wide.region_27.30_spmd.clone.clone, body=%wide.region_20.29_spmd.clone.clone.sunk | while | flops 53144164 | bytes 2176077 | solution.py:134
  181.1 7.8 %fusion.188 = (f32[32,128]{1,0:T(8,128)S(1)}, f32[32,128]{1,0:T(8,128)S(1)}, f32[32,128]{1,0:T(8,128)S(1)}, f32[32,128]{1,0:T(8,128)S(1)}, f32[32,128]{1,0:T(8,128)S(1)}, /*index=5*/f32[32,128]{1,0:T(8,128)S(1)}) fusion(f32[32,128]{1,0:T(8,128)S(1)} %bitcast.388, f32[32,128]{1,0:T(8,128)S(1)} %bitcast.400, f32[32,128]{1,0:T(8,128)S(1)} %bitcast.364, ...), kind=kLoop, calls=%fused_computation.137.clone.1 | loop fusion | flops 34054144 | bytes 344224 | tf_op jit(solution)/shard_map/while/body/eval_jaxpr/reduce_sum | solution.py:72
  196.9 7.8 %fusion.188 = (f32[32,128]{1,0:T(8,128)S(1)}, f32[32,128]{1,0:T(8,128)S(1)}, f32[32,128]{1,0:T(8,128)S(1)}, f32[32,128]{1,0:T(8,128)S(1)}, f32[32,128]{1,0:T(8,128)S(1)}, /*index=5*/f32[32,128]{1,0:T(8,128)S(1)}) fusion(f32[32,128]{1,0:T(8,128)S(1)} %bitcast.388, f32[32,128]{1,0:T(8,128)S(1)} %bitcast.400, f32[32,128]{1,0:T(8,128)S(1)} %bitcast.364, ...), kind=kLoop, calls=%fused_computation.137.clone.1 | loop fusion | flops 34054144 | bytes 344224 | tf_op jit(solution)/shard_map/while/body/eval_jaxpr/reduce_sum | solution.py:72
  212.7 7.8 %fusion.188 = (f32[32,128]{1,0:T(8,128)S(1)}, f32[32,128]{1,0:T(8,128)S(1)}, f32[32,128]{1,0:T(8,128)S(1)}, f32[32,128]{1,0:T(8,128)S(1)}, f32[32,128]{1,0:T(8,128)S(1)}, /*index=5*/f32[32,128]{1,0:T(8,128)S(1)}) fusion(f32[32,128]{1,0:T(8,128)S(1)} %bitcast.388, f32[32,128]{1,0:T(8,128)S(1)} %bitcast.400, f32[32,128]{1,0:T(8,128)S(1)} %bitcast.364, ...), kind=kLoop, calls=%fused_computation.137.clone.1 | loop fusion | flops 34054144 | bytes 344224 | tf_op jit(solution)/shard_map/while/body/eval_jaxpr/reduce_sum | solution.py:72
  221.4 2.2 collective-permute-done.4
  224.4 12.2 %all-reduce.6 = (f32[]{:T(128)}, f32[]{:T(128)}) all-reduce(f32[]{:T(128)} %get-tuple-element.757, f32[]{:T(128)} %get-tuple-element.756), channel_id=1, replica_groups=mesh['rep'=2,'gx_0'=8,'gx_1'=8,'gx_2'=2] {'gx_0'}, use_global_device_ids=true, to_apply=%region_17.20 | all-reduce | flops 2 | bytes 16 | tf_op jit(solution)/shard_map/psum | solution.py:19
  236.5 16.3 %all-reduce.2 = (f32[]{:T(128)}, f32[]{:T(128)}) all-reduce(f32[]{:T(128)} %get-tuple-element.860, f32[]{:T(128)} %get-tuple-element.861), channel_id=1, replica_groups=mesh['rep'=2,'gx_0'=8,'gx_1'=8,'gx_2'=2] {'gx_1'}, use_global_device_ids=true, to_apply=%region_18.21 | all-reduce | flops 2 | bytes 16 | tf_op jit(solution)/shard_map/psum | solution.py:19
  252.8 10.5 %all-reduce.10 = (f32[]{:T(128)}, f32[]{:T(128)}) all-reduce(f32[]{:T(128)} %get-tuple-element.852, f32[]{:T(128)} %get-tuple-element.853), channel_id=1, replica_groups=mesh['rep'=2,'gx_0'=8,'gx_1'=8,'gx_2'=2] {'gx_2'}, use_global_device_ids=true, to_apply=%region_19.22 | all-reduce | flops 2 | bytes 16 | tf_op jit(solution)/shard_map/psum | solution.py:19
  268.5 3.5 collective-permute-done.5
  272.1 46.8 %while.50 = (s32[]{:T(128)}, f32[64,384]{1,0:T(8,128)S(1)}, s32[3]{0:T(128)S(1)}, s32[96]{0:T(128)S(1)}, s32[96]{0:T(128)S(1)}, /*index=5*/s32[96]{0:T(128)S(1)}...) while((s32[]{:T(128)}, f32[64,384]{1,0:T(8,128)S(1)}, ...), condition=%wide.region_43.46_spmd.clone.clone, body=%wide.region_36.45_spmd.clone.clone.sunk | while | flops 53144164 | bytes 2176077 | solution.py:134
  279.2 7.8 %fusion.195 = (f32[32,128]{1,0:T(8,128)S(1)}, f32[32,128]{1,0:T(8,128)S(1)}, f32[32,128]{1,0:T(8,128)S(1)}, f32[32,128]{1,0:T(8,128)S(1)}, f32[32,128]{1,0:T(8,128)S(1)}, /*index=5*/f32[32,128]{1,0:T(8,128)S(1)}) fusion(f32[32,128]{1,0:T(8,128)S(1)} %bitcast.391, f32[32,128]{1,0:T(8,128)S(1)} %bitcast.403, f32[32,128]{1,0:T(8,128)S(1)} %bitcast.367, ...), kind=kLoop, calls=%fused_computation.208.clone.1 | loop fusion | flops 34054144 | bytes 344224 | tf_op jit(solution)/shard_map/while/body/eval_jaxpr/reduce_sum | solution.py:72
  294.8 7.8 %fusion.195 = (f32[32,128]{1,0:T(8,128)S(1)}, f32[32,128]{1,0:T(8,128)S(1)}, f32[32,128]{1,0:T(8,128)S(1)}, f32[32,128]{1,0:T(8,128)S(1)}, f32[32,128]{1,0:T(8,128)S(1)}, /*index=5*/f32[32,128]{1,0:T(8,128)S(1)}) fusion(f32[32,128]{1,0:T(8,128)S(1)} %bitcast.391, f32[32,128]{1,0:T(8,128)S(1)} %bitcast.403, f32[32,128]{1,0:T(8,128)S(1)} %bitcast.367, ...), kind=kLoop, calls=%fused_computation.208.clone.1 | loop fusion | flops 34054144 | bytes 344224 | tf_op jit(solution)/shard_map/while/body/eval_jaxpr/reduce_sum | solution.py:72
  310.4 7.8 %fusion.195 = (f32[32,128]{1,0:T(8,128)S(1)}, f32[32,128]{1,0:T(8,128)S(1)}, f32[32,128]{1,0:T(8,128)S(1)}, f32[32,128]{1,0:T(8,128)S(1)}, f32[32,128]{1,0:T(8,128)S(1)}, /*index=5*/f32[32,128]{1,0:T(8,128)S(1)}) fusion(f32[32,128]{1,0:T(8,128)S(1)} %bitcast.391, f32[32,128]{1,0:T(8,128)S(1)} %bitcast.403, f32[32,128]{1,0:T(8,128)S(1)} %bitcast.367, ...), kind=kLoop, calls=%fused_computation.208.clone.1 | loop fusion | flops 34054144 | bytes 344224 | tf_op jit(solution)/shard_map/while/body/eval_jaxpr/reduce_sum | solution.py:72
  319.1 2.2 collective-permute-done.6
  322.0 12.1 %all-reduce.5 = (f32[]{:T(128)}, f32[]{:T(128)}) all-reduce(f32[]{:T(128)} %get-tuple-element.755, f32[]{:T(128)} %get-tuple-element.754), channel_id=1, replica_groups=mesh['rep'=2,'gx_0'=8,'gx_1'=8,'gx_2'=2] {'gx_0'}, use_global_device_ids=true, to_apply=%region_33.36 | all-reduce | flops 2 | bytes 16 | tf_op jit(solution)/shard_map/psum | solution.py:19
  334.1 16.2 %all-reduce.1 = (f32[]{:T(128)}, f32[]{:T(128)}) all-reduce(f32[]{:T(128)} %get-tuple-element.858, f32[]{:T(128)} %get-tuple-element.859), channel_id=1, replica_groups=mesh['rep'=2,'gx_0'=8,'gx_1'=8,'gx_2'=2] {'gx_1'}, use_global_device_ids=true, to_apply=%region_34.37 | all-reduce | flops 2 | bytes 16 | tf_op jit(solution)/shard_map/psum | solution.py:19
  350.3 10.4 %all-reduce.9 = (f32[]{:T(128)}, f32[]{:T(128)}) all-reduce(f32[]{:T(128)} %get-tuple-element.850, f32[]{:T(128)} %get-tuple-element.851), channel_id=1, replica_groups=mesh['rep'=2,'gx_0'=8,'gx_1'=8,'gx_2'=2] {'gx_2'}, use_global_device_ids=true, to_apply=%region_35.38 | all-reduce | flops 2 | bytes 16 | tf_op jit(solution)/shard_map/psum | solution.py:19
  365.3 3.5 collective-permute-done.7
  368.9 47.5 %while.51 = (s32[]{:T(128)}, f32[64,384]{1,0:T(8,128)S(1)}, s32[3]{0:T(128)S(1)}, s32[96]{0:T(128)S(1)}, s32[96]{0:T(128)S(1)}, /*index=5*/s32[96]{0:T(128)S(1)}...) while((s32[]{:T(128)}, f32[64,384]{1,0:T(8,128)S(1)}, ...), condition=%wide.region_59.62_spmd.clone.clone, body=%wide.region_52.61_spmd.clone.clone.sunk | while | flops 53144164 | bytes 2176077 | solution.py:134
  376.3 7.8 %fusion.202 = (f32[32,128]{1,0:T(8,128)S(1)}, f32[32,128]{1,0:T(8,128)S(1)}, f32[32,128]{1,0:T(8,128)S(1)}, f32[32,128]{1,0:T(8,128)S(1)}, f32[32,128]{1,0:T(8,128)S(1)}, /*index=5*/f32[32,128]{1,0:T(8,128)S(1)}) fusion(f32[32,128]{1,0:T(8,128)S(1)} %bitcast.394, f32[32,128]{1,0:T(8,128)S(1)} %bitcast.406, f32[32,128]{1,0:T(8,128)S(1)} %bitcast.370, ...), kind=kLoop, calls=%fused_computation.279.clone.1 | loop fusion | flops 34054144 | bytes 344224 | tf_op jit(solution)/shard_map/while/body/eval_jaxpr/reduce_sum | solution.py:72
  392.1 7.8 %fusion.202 = (f32[32,128]{1,0:T(8,128)S(1)}, f32[32,128]{1,0:T(8,128)S(1)}, f32[32,128]{1,0:T(8,128)S(1)}, f32[32,128]{1,0:T(8,128)S(1)}, f32[32,128]{1,0:T(8,128)S(1)}, /*index=5*/f32[32,128]{1,0:T(8,128)S(1)}) fusion(f32[32,128]{1,0:T(8,128)S(1)} %bitcast.394, f32[32,128]{1,0:T(8,128)S(1)} %bitcast.406, f32[32,128]{1,0:T(8,128)S(1)} %bitcast.370, ...), kind=kLoop, calls=%fused_computation.279.clone.1 | loop fusion | flops 34054144 | bytes 344224 | tf_op jit(solution)/shard_map/while/body/eval_jaxpr/reduce_sum | solution.py:72
  407.9 7.8 %fusion.202 = (f32[32,128]{1,0:T(8,128)S(1)}, f32[32,128]{1,0:T(8,128)S(1)}, f32[32,128]{1,0:T(8,128)S(1)}, f32[32,128]{1,0:T(8,128)S(1)}, f32[32,128]{1,0:T(8,128)S(1)}, /*index=5*/f32[32,128]{1,0:T(8,128)S(1)}) fusion(f32[32,128]{1,0:T(8,128)S(1)} %bitcast.394, f32[32,128]{1,0:T(8,128)S(1)} %bitcast.406, f32[32,128]{1,0:T(8,128)S(1)} %bitcast.370, ...), kind=kLoop, calls=%fused_computation.279.clone.1 | loop fusion | flops 34054144 | bytes 344224 | tf_op jit(solution)/shard_map/while/body/eval_jaxpr/reduce_sum | solution.py:72
  416.6 2.2 collective-permute-done.8
  419.5 12.2 %all-reduce.4 = (f32[]{:T(128)}, f32[]{:T(128)}) all-reduce(f32[]{:T(128)} %get-tuple-element.753, f32[]{:T(128)} %get-tuple-element.752), channel_id=1, replica_groups=mesh['rep'=2,'gx_0'=8,'gx_1'=8,'gx_2'=2] {'gx_0'}, use_global_device_ids=true, to_apply=%region_49.52 | all-reduce | flops 2 | bytes 16 | tf_op jit(solution)/shard_map/psum | solution.py:19
  431.6 16.2 %all-reduce = (f32[]{:T(128)}, f32[]{:T(128)}) all-reduce(f32[]{:T(128)} %get-tuple-element.856, f32[]{:T(128)} %get-tuple-element.857), channel_id=1, replica_groups=mesh['rep'=2,'gx_0'=8,'gx_1'=8,'gx_2'=2] {'gx_1'}, use_global_device_ids=true, to_apply=%region_50.53 | all-reduce | flops 2 | bytes 16 | tf_op jit(solution)/shard_map/psum | solution.py:19
  447.9 10.5 %all-reduce.8 = (f32[]{:T(128)}, f32[]{:T(128)}) all-reduce(f32[]{:T(128)} %get-tuple-element.848, f32[]{:T(128)} %get-tuple-element.849), channel_id=1, replica_groups=mesh['rep'=2,'gx_0'=8,'gx_1'=8,'gx_2'=2] {'gx_2'}, use_global_device_ids=true, to_apply=%region_51.54 | all-reduce | flops 2 | bytes 16 | tf_op jit(solution)/shard_map/psum | solution.py:19
  462.6 2.0 copy.101
  464.6 11.6 %scatter_custom_fusion.1 = f32[3,4096]{0,1:T(8,128)S(1)} fusion(s32[4096]{0:T(1024)S(1)} %get-tuple-element.976, f32[4096,3]{1,0:T(8,128)} %copy.101, f32[]{:T(128)} %constant.22.clone.1), kind=kCustom, calls=%fused_computation.317 | custom fusion | bytes 49664 | tf_op jit(solution)/shard_map/scatter | solution.py:220
  476.2 1.2 copy.103
  477.5 2.0 copy.100
  479.5 11.4 %scatter_custom_fusion = f32[3,4096]{0,1:T(8,128)S(1)} fusion(s32[4096]{0:T(1024)S(1)} %get-tuple-element.976, f32[4096,3]{1,0:T(8,128)} %copy.100, f32[]{:T(128)} %constant.22.clone.1), kind=kCustom, calls=%fused_computation.319 | custom fusion | bytes 49664 | tf_op jit(solution)/shard_map/scatter | solution.py:215
  490.9 1.2 copy.102
  (401 shorter events, 78.1 us)
Async XLA Ops:
  0.6 0.7 copy-start
  1.4 23.1 %copy-start.1 = (f32[3,4096]{1,0:T(4,128)S(1)}, f32[3,4096]{1,0:T(4,128)}, u32[]{:S(2)}) copy-start(f32[3,4096]{1,0:T(4,128)} %param.18) | copy-start | bytes 147460
  24.5 37.5 %copy-start.2 = (f32[3,4096]{1,0:T(4,128)S(1)}, f32[3,4096]{1,0:T(4,128)}, u32[]{:S(2)}) copy-start(f32[3,4096]{1,0:T(4,128)} %param.20) | copy-start | bytes 147460
  41.4 37.6 %copy-start.3 = (s32[32,3]{0,1:T(4,128)S(1)}, s32[32,3]{0,1:T(4,128)}, u32[]{:S(2)}) copy-start(s32[32,3]{0,1:T(4,128)} %param.22) | copy-start | bytes 1156
  41.4 37.8 %copy-start.4 = (s32[2,32,3]{1,0,2:T(2,128)S(1)}, s32[2,32,3]{1,0,2:T(2,128)}, u32[]{:S(2)}) copy-start(s32[2,32,3]{1,0,2:T(2,128)} %param.23) | copy-start | bytes 2308
  41.4 41.3 %collective-permute-start = (f32[32,4,128]{2,0,1:T(8,128)S(1)}, f32[32,4,128]{2,0,1:T(8,128)S(1)}, u32[]{:S(2)}, u32[]{:S(2)}) collective-permute-start(f32[32,4,128]{2,0,1:T(8,128)S(1)} %pad_maximum_fusion.5), channel_id=1, source_target_pairs={{0,127},{1,0},{2,1},{3,2},{4,3},{5,4},{6,5},{7,6},{8,7},{9,8},{10,... | collective-permute-start | bytes 196616 | tf_op jit(solution)/shard_map/ppermute | solution.py:25
  78.9 3.8 collective-permute-start.1
  129.7 1.5 collective-permute-start.2
  169.7 4.0 collective-permute-start.3
  221.2 2.4 collective-permute-start.4
  268.0 4.0 collective-permute-start.5
  318.9 2.4 collective-permute-start.6
  364.9 4.0 collective-permute-start.7
  416.4 2.4 collective-permute-start.8
where the time goes:
time: 493 us; the launch traced here: 492 us
  blocking collectives  153 us (31%)
  local copies, waits for them, and re-layouts  143 us (29%)
  other arithmetic  104 us (21%)
  loops' own time  25.6 us (5%)
  starting transfers between devices  22.5 us (5%)
  waiting for transfers between devices  21.1 us (4%)
  between operations  15.3 us (3%)
  matrix products  7.52 us (2%)
    psum x12, blocking collectives, over_axes(): return functools.reduce(lax.psum, axes, shard)  153 us
    reduce_sum x12, other arithmetic, pair_block(): jnp.sum(lift_left * offsets[component] - coeff_three * moment_left[:, com...  93.5 us
    another operation x4, loops' own time, slab_fields(): lax.scan(accumulate, jnp.zeros((window_size, 3 * tile_width), jnp.float32...  25.6 us
    gather x1, local copies, waits for them, and re-layouts, on_device(): tiled_polar = polar[tile_atom].reshape(tile_count, tile_width)  23 us
    ppermute x9, starting transfers between devices, passed_along(): return lax.ppermute(value, axis, pairs)  22.5 us
    ppermute x9, waiting for transfers between devices, passed_along(): return lax.ppermute(value, axis, pairs)  21.1 us
    gather x1, local copies, waits for them, and re-layouts, on_device(): positions[:, tile_atom].reshape(3, tile_count, tile_width)  14.1 us
    gather x1, local copies, waits for them, and re-layouts, on_device(): field_ext[:, tile_atom].reshape(3, tile_count, tile_width)  14.1 us
  transfers between devices with their start and end apart: 9, of which 8 were waited for; matrix products, arithmetic and copies ran while one was open for 4% of the time, Pallas kernels for 0%

commit v1 on v0

v1 whole, which is shorter than its diff:
```python
import functools

import jax
import jax.numpy as jnp
from jax import lax
from jax.experimental import pallas as pl
from jax.experimental.pallas import tpu as pltpu
from jax.sharding import PartitionSpec as P

ITERS = 4
REP_GX = ("rep", "gx")
THOLE = 0.39
SHIFT = 2.5
SCALE = 1.5
MATS = 4
SLOTS = 10
MIB = 2**20

F32 = jnp.float32
VMEM = pl.BlockSpec(memory_space=pltpu.VMEM)
SMEM = pl.BlockSpec(memory_space=pltpu.SMEM)
HBM = pl.BlockSpec(memory_space=pltpu.MemorySpace.HBM)


def spread(row, height=8):
    return jnp.broadcast_to(row, (height, row.shape[1]))


def lane_pick(row_block, lanes):
    return jnp.take_along_axis(row_block, lanes, axis=1)


def params(mib):
    return pltpu.CompilerParams(vmem_limit_bytes=mib * MIB)


def tile_in_kernel(pos_ref, pol_ref, fld_ref, idx_ref, out_ref):
    tiles = idx_ref.shape[0]
    width = idx_ref.shape[1]
    for q in range(tiles // 8):
        rows = idx_ref[8 * q : 8 * q + 8, :]
        high = rows // width
        low = rows - high * width

        def step(h, acc):
            at = pl.ds(pl.multiple_of(h * width, width), width)
            hit = high == h
            new = []
            for c in range(7):
                if c < 3:
                    row = pos_ref[c : c + 1, at]
                elif c == 3:
                    row = pol_ref[0:1, at]
                else:
                    row = fld_ref[c - 4 : c - 3, at]
                new.append(jnp.where(hit, lane_pick(spread(row), low), acc[c]))
            return tuple(new)

        acc = lax.fori_loop(0, tiles, step, (jnp.zeros((8, width), F32),) * 7, unroll=4)
        values = list(acc[:3]) + [lax.rsqrt(acc[3])] + list(acc[4:]) + [1.0 / acc[3]]
        for c in range(8):
            out_ref[c * tiles + 8 * q : c * tiles + 8 * q + 8, :] = values[c]


def inverse_kernel(idx_ref, out_ref):
    tiles, width = idx_ref.shape
    total = jnp.zeros((2 * tiles, width), F32)
    lane = lax.broadcasted_iota(jnp.int32, (tiles, width), 1).astype(F32)
    row_id = lax.broadcasted_iota(jnp.int32, (tiles, width), 0)
    low_id = lax.broadcasted_iota(jnp.int32, (width, width), 0)
    for t in range(tiles):
        row = idx_ref[t : t + 1, :]
        high = row // width
        low = row - high * width
        hit = spread(high, tiles) == row_id
        left = jnp.concatenate([jnp.where(hit, float(t), 0.0), jnp.where(hit, lane, 0.0)], axis=0)
        right = jnp.where(spread(low, width) == low_id, 1.0, 0.0)
        total = total + lax.dot_general(
            left.astype(jnp.bfloat16),
            right.astype(jnp.bfloat16),
            (((1,), (1,)), ((), ())),
            preferred_element_type=F32,
        )
    out_ref[...] = (total[:tiles] * float(width) + total[tiles:] + 0.5).astype(jnp.int32)


def take_neighbours(par, near_ref, far_ref, nb_ref, start, rows):
    nb_ref[pl.ds(pl.multiple_of(par * rows, 8), rows), :] = near_ref[start : start + rows, :]
    nb_ref[pl.ds(pl.multiple_of((1 - par) * rows, 8), rows), :] = far_ref[start : start + rows, :]


def pair_coefficients(off, ci, rj, same):
    dist_sq = off[0] * off[0] + off[1] * off[1] + off[2] * off[2]
    if same is not None:
        dist_sq = jnp.where(same, 1.0, dist_sq)
    inv = lax.rsqrt(dist_sq)
    damp = (dist_sq * (dist_sq * inv)) * (ci * rj)
    decay = jnp.exp(-damp)
    inv_sq = inv * inv
    cube = inv_sq * inv
    g3 = (1.0 - decay) * cube
    g5 = (3.0 - (3.0 + 3.0 * damp) * decay) * (cube * inv_sq)
    root = g5 * lax.rsqrt(g5)
    if same is not None:
        g3 = jnp.where(same, 0.0, g3)
        root = jnp.where(same, 0.0, root)
    return [root * off[0], root * off[1], root * off[2], g3]


def pairs_kernel(
    par_ref, own_list, prev_list, own_ref, near_ref, far_ref,
    tensor_ref, prev_hbm, tab_ref, nb_ref, col_ref, out_slots, sems,
    *, boxes,
):
    tiles = own_ref.shape[0] // 8
    width = own_ref.shape[1]
    par = par_ref[0]
    wrap_next = par_ref[1].astype(F32) * boxes[0]
    wrap_prev = par_ref[2].astype(F32) * boxes[0]
    rows = 4 * tiles
    take_neighbours(par, near_ref, far_ref, nb_ref, 0, rows)
    links = own_list.shape[1] // tiles
    extra = links - 1
    cap = extra * tiles

    def sort_own(k, counts):
        inner, outer = counts
        t = k // extra
        at = t * links + 1 + (k - t * extra)
        n = own_list[0, at]
        tab_ref[1, inner] = k
        tab_ref[2, outer] = k
        near = (n < tiles).astype(jnp.int32)
        return inner + near, outer + 1 - near

    inner, outer = lax.fori_loop(0, cap, sort_own, (jnp.int32(0), jnp.int32(0)))

    def sort_prev(k, count):
        t = k // extra
        at = t * links + 1 + (k - t * extra)
        n = prev_list[0, at]
        tab_ref[3, count] = k
        return count + (n >= tiles).astype(jnp.int32)

    behind = lax.fori_loop(0, cap, sort_prev, jnp.int32(0))
    tab_ref[0, 0] = inner
    tab_ref[0, 1] = outer
    tab_ref[0, 2] = behind

    def columns(t, _):
        for c in range(4):
            row = own_ref[pl.ds(c * tiles + t, 1), :]
            if c == 3:
                row = row * THOLE
            col_ref[pl.ds(pl.multiple_of((t * 4 + c) * width, width), width), :] = spread(row, width).T
        return 0

    lax.fori_loop(0, tiles, columns, 0)
    chunks = width // 8

    def block(own_tile, row, store, same, lead):
        for k in range(chunks):
            base = pl.multiple_of(own_tile * 4 * width, width)
            col = [col_ref[pl.ds(base + c * width + 8 * k, 8), :] for c in range(4)]
            if lead is not None:
                off = [(col[c] + lead[c]) - row[c] for c in range(3)]
            else:
                off = [row[c] - col[c] for c in range(3)]
            mask = None
            if same:
                i = lax.broadcasted_iota(jnp.int32, (8, width), 0) + 8 * k
                j = lax.broadcasted_iota(jnp.int32, (8, width), 1)
                mask = i == j
            store(k, pair_coefficients(off, col[3], row[3], mask))

    def store_own(slot):
        def store(k, mats):
            for m in range(MATS):
                at = pl.multiple_of((slot * MATS + m) * width, width) + 8 * k
                tensor_ref[pl.ds(at, 8), :] = mats[m]

        return store

    def own_rows(n):
        return [spread(own_ref[pl.ds(c * tiles + n, 1), :]) for c in range(4)]

    def nb_rows(side, n):
        return [spread(nb_ref[pl.ds(side * rows + c * tiles + n, 1), :]) for c in range(4)]

    def self_job(t, _):
        block(t, own_rows(t), store_own(t), True, None)
        return 0

    lax.fori_loop(0, tiles, self_job, 0)

    def shifts(lists, at):
        return lists[1, at].astype(F32) * boxes[1], lists[2, at].astype(F32) * boxes[2]

    def shifted(row, lead):
        return [row[c] + lead[c] for c in range(3)] + [row[3]]

    def inner_job(i, _):
        k = tab_ref[1, i]
        t = k // extra
        at = t * links + 1 + (k - t * extra)
        n = own_list[0, at]
        y, z = shifts(own_list, at)
        block(t, shifted(own_rows(n), (0.0, y, z)), store_own(tiles + k), False, None)
        return 0

    lax.fori_loop(0, inner, inner_job, 0)

    def outer_job(i, _):
        k = tab_ref[2, i]
        t = k // extra
        at = t * links + 1 + (k - t * extra)
        n = own_list[0, at] - tiles
        y, z = shifts(own_list, at)
        block(t, shifted(nb_rows(0, n), (wrap_next, y, z)), store_own(tiles + k), False, None)
        return 0

    lax.fori_loop(0, outer, outer_job, 0)

    def out_copy(i):
        slot = lax.rem(i, 2)
        size = MATS * width
        return pltpu.make_async_copy(
            out_slots.at[pl.ds(pl.multiple_of(slot * size, size), size), :],
            prev_hbm.at[pl.ds(pl.multiple_of(i * size, size), size), :],
            sems.at[slot],
        )

    def behind_job(i, _):
        k = tab_ref[3, i]
        t = k // extra
        at = t * links + 1 + (k - t * extra)
        n = prev_list[0, at] - tiles
        y, z = shifts(prev_list, at)

        @pl.when(i >= 2)
        def _():
            out_copy(i - 2).wait()

        base = pl.multiple_of(lax.rem(i, 2) * MATS * width, width)

        def store(c, mats):
            for m in range(MATS):
                out_slots[pl.ds(base + m * width + 8 * c, 8), :] = mats[m]

        block(n, nb_rows(1, t), store, False, (wrap_prev, y, z))
        out_copy(i).start()
        return 0

    lax.fori_loop(0, behind, behind_job, 0)

    @pl.when(behind >= 2)
    def _():
        out_copy(behind - 2).wait()

    @pl.when(behind >= 1)
    def _():
        out_copy(behind - 1).wait()


def apply_kernel(
    par_ref, tab_ref, own_list, prev_list, tensor_ref, prev_hbm, own_ref, near_ref, far_ref, inv_ref,
    out_ref, nb_ref, left_ref, right_ref, slots_ref, sems,
    *, start, inv_start,
):
    width = own_ref.shape[1]
    rows = out_ref.shape[0]
    tiles = rows // 3
    links = own_list.shape[1] // tiles
    extra = links - 1
    par = par_ref[0]
    inner = tab_ref[0, 0]
    outer = tab_ref[0, 1]
    behind = tab_ref[0, 2]
    chunks = width // 8
    size = MATS * width

    def in_copy(i):
        slot = lax.rem(i, SLOTS)
        return pltpu.make_async_copy(
            prev_hbm.at[pl.ds(pl.multiple_of(i * size, size), size), :],
            slots_ref.at[pl.ds(pl.multiple_of(slot * size, size), size), :],
            sems.at[slot],
        )

    def begin(i, _):
        in_copy(i).start()
        return 0

    lax.fori_loop(0, jnp.minimum(behind, SLOTS), begin, 0)
    take_neighbours(par, near_ref, far_ref, nb_ref, start, rows)
    right_ref[...] = jnp.zeros_like(right_ref)

    def own_rows(n):
        return [spread(own_ref[pl.ds(start + c * tiles + n, 1), :]) for c in range(3)]

    def nb_rows(side, n):
        return [spread(nb_ref[pl.ds(side * rows + c * tiles + n, 1), :]) for c in range(3)]

    def left_at(tile, c, k):
        return pl.ds(pl.multiple_of((tile * 3 + c) * width, width) + 8 * k, 8)

    def one_side(source, base, tile, row, fresh):
        for k in range(chunks):
            s = [source[pl.ds(base + m * width + 8 * k, 8), :] for m in range(MATS)]
            lift = s[0] * row[0] + s[1] * row[1] + s[2] * row[2]
            for c in range(3):
                value = s[c] * lift - s[3] * row[c]
                if not fresh:
                    value = left_ref[left_at(tile, c, k), :] + value
                left_ref[left_at(tile, c, k), :] = value

    def self_job(t, _):
        one_side(tensor_ref, pl.multiple_of(t * size, size), t, own_rows(t), True)
        return 0

    lax.fori_loop(0, tiles, self_job, 0)

    def inner_job(i, _):
        k = tab_ref[1, i]
        t = k // extra
        n = own_list[0, t * links + 1 + (k - t * extra)]
        base = pl.multiple_of((tiles + k) * size, size)
        row = own_rows(n)
        col = [spread(own_ref[pl.ds(start + c * tiles + t, 1), :], width).T for c in range(3)]
        acc = [right_ref[pl.ds(pl.multiple_of((n * 3 + c) * 8, 8), 8), :] for c in range(3)]
        for q in range(chunks):
            s = [tensor_ref[pl.ds(base + m * width + 8 * q, 8), :] for m in range(MATS)]
            lift = s[0] * row[0] + s[1] * row[1] + s[2] * row[2]
            for c in range(3):
                at = left_at(t, c, q)
                left_ref[at, :] = left_ref[at, :] + (s[c] * lift - s[3] * row[c])
            mine = [col[c][8 * q : 8 * q + 8, :] for c in range(3)]
            lift = s[0] * mine[0] + s[1] * mine[1] + s[2] * mine[2]
            for c in range(3):
                acc[c] = acc[c] + (s[c] * lift - s[3] * mine[c])
        for c in range(3):
            right_ref[pl.ds(pl.multiple_of((n * 3 + c) * 8, 8), 8), :] = acc[c]
        return 0

    lax.fori_loop(0, inner, inner_job, 0)

    def outer_job(i, _):
        k = tab_ref[2, i]
        t = k // extra
        n = own_list[0, t * links + 1 + (k - t * extra)] - tiles
        one_side(tensor_ref, pl.multiple_of((tiles + k) * size, size), t, nb_rows(0, n), False)
        return 0

    lax.fori_loop(0, outer, outer_job, 0)

    def behind_job(i, _):
        k = tab_ref[3, i]
        t = k // extra
        n = prev_list[0, t * links + 1 + (k - t * extra)] - tiles
        in_copy(i).wait()
        slot = lax.rem(i, SLOTS)
        one_side(slots_ref, pl.multiple_of(slot * size, size), n, nb_rows(1, t), False)

        @pl.when(i + SLOTS < behind)
        def _():
            in_copy(i + SLOTS).start()

        return 0

    lax.fori_loop(0, behind, behind_job, 0)

    def finish(t, _):
        weight = (inv_ref[pl.ds(inv_start + t, 1), :] - SHIFT) * (1.0 / SCALE)
        for c in range(3):
            block = left_ref[pl.ds(pl.multiple_of((t * 3 + c) * width, width), width), :].T
            field = jnp.sum(block, axis=0, keepdims=True) + jnp.sum(
                right_ref[pl.ds(pl.multiple_of((t * 3 + c) * 8, 8), 8), :], axis=0, keepdims=True
            )
            mine = own_ref[pl.ds(start + c * tiles + t, 1), :]
            out_ref[pl.ds(c * tiles + t, 1), :] = mine * weight - field * (1.0 / SCALE)
        return 0

    lax.fori_loop(0, tiles, finish, 0, unroll=2)


PAIRS = [(i, j) for i in range(ITERS + 1) for j in range(i, ITERS + 1)]


def gram_kernel(*refs, start):
    vectors, out_ref = refs[:-1], refs[-1]
    rows, width = vectors[-1].shape
    lane = lax.broadcasted_iota(jnp.int32, (1, width), 1)
    total = jnp.zeros((1, width), F32)
    starts = (start,) + (0,) * ITERS
    for n, (i, j) in enumerate(PAIRS):
        product = vectors[i][starts[i] : starts[i] + rows, :] * vectors[j][starts[j] : starts[j] + rows, :]
        line = jnp.sum(product, axis=0, keepdims=True)
        total = jnp.where(lane == n, jnp.sum(line, axis=1, keepdims=True), total)
    out_ref[...] = total


def output_kernel(parts_ref, inv_ref, *refs, start):
    vectors, (dip_ref, res_ref, mix_ref) = refs[: ITERS + 1], refs[ITERS + 1 :]
    rows, width = vectors[-1].shape
    tiles = rows // 3
    sums = jnp.sum(parts_ref[...], axis=0, keepdims=True)
    lane = lax.broadcasted_iota(jnp.int32, (1, width), 1)
    gram = {}
    for n, (i, j) in enumerate(PAIRS):
        value = jnp.sum(jnp.where(lane == n, sums, 0.0), axis=1, keepdims=True)
        gram[i, j] = gram[j, i] = jnp.broadcast_to(value, (8, width))
    zero = jnp.zeros((8, width), F32)

    def add(a, b):
        return b if a is None else a if b is None else a + b

    def inner(a, b):
        total = None
        for i in range(ITERS + 1):
            for j in range(ITERS + 1):
                if a[i] is not None and b[j] is not None:
                    total = add(total, a[i] * b[j] * gram[i, j])
        return total

    def operate(a):
        out = [None if v is None else SHIFT * v for v in a]
        for i in range(ITERS):
            if a[i] is not None:
                out[i + 1] = add(out[i + 1], SCALE * a[i])
        return out

    x = [None] * (ITERS + 1)
    r = [zero + 1.0] + [None] * ITERS
    d = list(r)
    norm = inner(r, r)
    for step in range(ITERS):
        q = operate(d)
        size = norm / inner(d, q)
        x = [add(x[k], None if d[k] is None else size * d[k]) for k in range(ITERS + 1)]
        r = [add(r[k], None if q[k] is None else -size * q[k]) for k in range(ITERS + 1)]
        if step + 1 < ITERS:
            new = inner(r, r)
            ratio = new / norm
            d = [add(r[k], None if d[k] is None else ratio * d[k]) for k in range(ITERS + 1)]
            norm = new
    starts = (start,) + (0,) * ITERS
    for b in range(rows // 8):
        for which, weights in enumerate((x, r)):
            total = None
            for k in range(ITERS + 1):
                if weights[k] is not None:
                    total = add(total, weights[k] * vectors[k][starts[k] + 8 * b : starts[k] + 8 * b + 8, :])
            mix_ref[which * rows + 8 * b : which * rows + 8 * b + 8, :] = total
    for q in range(tiles // 8):
        index = inv_ref[8 * q : 8 * q + 8, :]
        high = index // width
        low = index - high * width

        def step(h, acc):
            hit = high == h
            return tuple(
                jnp.where(hit, lane_pick(spread(mix_ref[pl.ds(c * tiles + h, 1), :]), low), acc[c])
                for c in range(6)
            )

        acc = lax.fori_loop(0, tiles, step, (zero,) * 6, unroll=4)
        for c in range(6):
            out = dip_ref if c < 3 else res_ref
            for s in range(8):
                at = (8 * q + s) * width
                out[c % 3 : c % 3 + 1, at : at + width] = acc[c][s : s + 1, :]


def shape(rows, width, dtype=F32):
    return jax.ShapeDtypeStruct((rows, width), dtype)


def on_device(positions, polar, field_ext, tile_atom, tile_list, image_shift):
    tiles, links = tile_list.shape
    atoms = tile_atom.shape[0]
    width = atoms // tiles
    slabs = lax.axis_size("gx")
    slab = lax.axis_index("gx")
    rows = 3 * tiles
    cap = tiles * (links - 1)
    boxes = (4.0 * slabs, 128.0, 2.0 * tiles)
    near_pairs = [(i, i ^ 1) for i in range(slabs)]
    far_pairs = [(i, ((i + 1) ^ 1) - 1 if 0 < i < slabs - 1 else slabs - 1 - i) for i in range(slabs)]

    def swap(value):
        return lax.ppermute(value, "gx", near_pairs), lax.ppermute(value, "gx", far_pairs)

    lists = jnp.concatenate(
        [tile_list.reshape(1, -1), image_shift.reshape(2, -1)], axis=0
    )
    prev_lists = lax.ppermute(lists, "gx", [(i, (i + 1) % slabs) for i in range(slabs)])
    par = jnp.stack(
        [slab % 2, (slab == slabs - 1).astype(jnp.int32), (slab == 0).astype(jnp.int32)]
    ).astype(jnp.int32)
    index = tile_atom.reshape(tiles, width)
    packed = pl.pallas_call(
        tile_in_kernel,
        out_shape=shape(8 * tiles, width),
        in_specs=[VMEM] * 4,
        out_specs=VMEM,
        compiler_params=params(4),
        name="tile_in",
    )(positions, polar.reshape(1, -1), field_ext, index)
    inverse = pl.pallas_call(
        inverse_kernel,
        out_shape=shape(tiles, width, jnp.int32),
        in_specs=[VMEM],
        out_specs=VMEM,
        compiler_params=params(4),
        cost_estimate=pl.CostEstimate(flops=4_000_000, bytes_accessed=32768, transcendentals=0),
        name="inverse",
    )(index)
    near, far = swap(packed)
    tensor, prev_tensor, table = pl.pallas_call(
        functools.partial(pairs_kernel, boxes=boxes),
        out_shape=(
            pltpu.VMEM(((tiles + cap) * MATS * width, width), F32),
            pltpu.MemorySpace.HBM((cap * MATS * width, width), F32),
            shape(4, cap + 1, jnp.int32),
        ),
        in_specs=[SMEM] * 3 + [VMEM] * 3,
        out_specs=(VMEM, HBM, SMEM),
        scratch_shapes=[
            pltpu.VMEM((2 * 4 * tiles, width), F32),
            pltpu.VMEM((4 * tiles * width, width), F32),
            pltpu.VMEM((2 * MATS * width, width), F32),
            pltpu.SemaphoreType.DMA((2,)),
        ],
        compiler_params=params(10),
        name="pairs",
    )(par, lists, prev_lists, packed, near, far)

    prev_tensor = pltpu.with_memory_space_constraint(prev_tensor, pltpu.MemorySpace.HBM)

    def apply(vector, near, far, start):
        return pl.pallas_call(
            functools.partial(apply_kernel, start=start, inv_start=7 * tiles),
            out_shape=shape(rows, width),
            in_specs=[SMEM] * 4 + [VMEM, HBM] + [VMEM] * 4,
            out_specs=VMEM,
            scratch_shapes=[
                pltpu.VMEM((2 * rows, width), F32),
                pltpu.VMEM((rows * width, width), F32),
                pltpu.VMEM((8 * rows, width), F32),
                pltpu.VMEM((SLOTS * MATS * width, width), F32),
                pltpu.SemaphoreType.DMA((SLOTS,)),
            ],
            compiler_params=params(10),
            name="apply",
        )(par, table, lists, prev_lists, tensor, prev_tensor, vector, near, far, packed)

    start = 4 * tiles
    basis = [packed]
    vector = apply(packed, near, far, start)
    basis.append(vector)
    for _ in range(ITERS - 1):
        near, far = swap(vector)
        vector = apply(vector, near, far, 0)
        basis.append(vector)
    gram = pl.pallas_call(
        functools.partial(gram_kernel, start=start),
        out_shape=shape(1, width),
        in_specs=[VMEM] * (ITERS + 1),
        out_specs=VMEM,
        compiler_params=params(4),
        name="gram",
    )(*basis)
    parts = lax.all_to_all(jnp.broadcast_to(gram, (slabs, width)), "gx", 0, 0, tiled=True)
    return pl.pallas_call(
        functools.partial(output_kernel, start=start),
        out_shape=(shape(3, atoms), shape(3, atoms)),
        in_specs=[VMEM] * (ITERS + 3),
        out_specs=(VMEM, VMEM),
        scratch_shapes=[pltpu.VMEM((2 * rows, width), F32)],
        compiler_params=params(4),
        name="outputs",
    )(parts, inverse, *basis)


def solution(mesh):
    return jax.shard_map(
        on_device,
        mesh=mesh,
        in_specs=(
            P(None, REP_GX),
            P(REP_GX),
            P(None, REP_GX),
            P(REP_GX),
            P(REP_GX, None),
            P(None, REP_GX, None),
        ),
        out_specs=(P(None, REP_GX), P(None, REP_GX)),
        check_vma=False,
    )
```

time: 493 us -> 178 us (0.36)
  blocking collectives: 153 us -> 0 us
  local copies, waits for them, and re-layouts: 143 us -> 5.53 us
  other arithmetic: 104 us -> 0.08 us
  Pallas kernels: 0 us -> 95.8 us
  starting transfers between devices: 22.5 us -> 50.9 us
  loops' own time: 25.6 us -> 0 us
  between operations: 15.3 us -> 0.75 us
  matrix products: 7.52 us -> 0 us
    psum x12 -> x0, blocking collectives: 153 us -> none  [over_axes(): return functools.reduce(lax.psum, axes, shard)]
    reduce_sum x16 -> x0, other arithmetic: 96.2 us -> none  [the longest x12 93.5 us: pair_block(): jnp.sum(lift_left * offsets[component] - coeff_three * moment_left[:, com...]
    pallas_call x0 -> x9, Pallas kernels: none -> 95.8 us  [the longest x4 57.7 us: apply(): pl.pallas_call(functools.partial(apply_kernel, start=start, inv_start=7 *...]
    gather x75 -> x0, local copies, waits for them, and re-layouts: 94.2 us -> none  [the longest x1 23 us: on_device(): tiled_polar = polar[tile_atom].reshape(tile_count, tile_width)]
    another operation x4 -> x0, loops' own time: 25.6 us -> none  [slab_fields(): lax.scan(accumulate, jnp.zeros((window_size, 3 * tile_width), jnp.float32...]
    scatter x2 -> x0, local copies, waits for them, and re-layouts: 23.1 us -> none  [the longest x1 11.6 us: on_device(): residual = jnp.zeros((3, atom_count), jnp.float32).at[:, tile_atom].set(r...]
    ppermute x9, starting transfers between devices: 22.5 us -> 39.2 us  [the longest x4 37.4 us: swap(): lax.ppermute(value, 'gx', near_pairs)]
    all_to_all x0 -> x1, starting transfers between devices: none -> 11.7 us  [on_device(): lax.all_to_all(jnp.broadcast_to(gram, (slabs, width)), 'gx', 0, 0, tiled=...]
  transfers between devices with their start and end apart: 9 -> 10, of which waited for: 8 -> 8; matrix products, arithmetic and copies ran while one was open for 4% -> 1% of each run, Pallas kernels for 0% -> 0%
where the time goes in v1:
time: 178 us; the launch traced here: 176 us
  Pallas kernels  95.8 us (54%)
  starting transfers between devices  50.9 us (29%)
  waiting for transfers between devices  22.6 us (13%)
  local copies, waits for them, and re-layouts  5.53 us (3%)
    pallas_call x4, Pallas kernels, apply(): pl.pallas_call(functools.partial(apply_kernel, start=start, inv_start=7 *...  57.7 us
    ppermute x4, starting transfers between devices, swap(): lax.ppermute(value, 'gx', near_pairs)  37.4 us
    pallas_call x1, Pallas kernels, on_device(): pl.pallas_call(functools.partial(pairs_kernel, boxes=boxes), out_shape=(p...  29.9 us
    all_to_all x1, starting transfers between devices, on_device(): lax.all_to_all(jnp.broadcast_to(gram, (slabs, width)), 'gx', 0, 0, tiled=...  11.7 us
    all_to_all x1, waiting for transfers between devices, on_device(): lax.all_to_all(jnp.broadcast_to(gram, (slabs, width)), 'gx', 0, 0, tiled=...  11.4 us
    ppermute x4, waiting for transfers between devices, swap(): lax.ppermute(value, 'gx', far_pairs)  7.93 us
    unnamed x12, local copies, waits for them, and re-layouts  4.65 us
    pallas_call x1, Pallas kernels, on_device(): pl.pallas_call(functools.partial(output_kernel, start=start), out_shape=(...  4.03 us
  transfers between devices with their start and end apart: 10, of which 8 were waited for; matrix products, arithmetic and copies ran while one was open for 1% of the time, Pallas kernels for 0%

profile of v1, /device:TPU:513, one launch (start us, length us, event | category | flops | bytes accessed | tf_op | source)
XLA Modules:
  0.0 175.7 jit_solution(2972876373902472994)
XLA Ops:
  0.6 0.0 copy-start
  0.6 0.7 copy-done
  1.4 0.0 copy-start.2
  1.4 0.8 copy-done.2
  2.2 0.0 copy-start.3
  2.2 0.8 copy-done.3
  3.0 0.0 copy-start.4
  3.0 0.7 copy-done.4
  3.7 3.2 %tile_in.1.own_ref.inv_ref.refs_0_ = f32[256,128]{1,0:T(8,128)S(1)} custom-call(f32[3,4096]{1,0:T(4,128)S(1)} %copy-done.2, f32[1,4096]{1,0:T(1,128)S(1)} %bitcast.10, f32[3,4096]{1,0:T(4,128)S(1)} %copy-done.3, s32[32,128]{1,0:T(8,128)S(1)} %bitcast.8), custom_call_target="tpu_custom_call" | custom-call | tf_op jit(solution)/shard_map/tile_in/pallas_call | solution.py:501
  7.0 20.5 %collective-permute-start.1 = (f32[256,128]{1,0:T(8,128)S(1)}, f32[256,128]{1,0:T(8,128)S(1)}, u32[]{:S(2)}, u32[]{:S(2)}) collective-permute-start(f32[256,128]{1,0:T(8,128)S(1)} %tile_in.1.own_ref.inv_ref.refs_0_), channel_id=1, source_target_pairs={{0,1},{1,0},{2,3},{3,2},{4,5},{5,4},{6,7},{7,6},{8,9},{9,8},{10,11... | collective-permute-start | bytes 393224 | tf_op jit(solution)/shard_map/ppermute | solution.py:491
  27.5 0.0 collective-permute-start.2
  27.5 0.8 copy.13
  28.3 0.1 reshape.25
  28.4 0.8 copy.12
  29.2 0.1 reshape.24
  29.3 1.9 %collective-permute-start = (s32[3,96]{1,0:T(4,128)S(1)}, s32[3,96]{1,0:T(4,128)S(1)}, u32[]{:S(2)}, u32[]{:S(2)}) collective-permute-start(s32[3,96]{1,0:T(4,128)S(1)} %pad_add_fusion.own_list), channel_id=1, source_target_pairs={{0,1},{1,2},{2,3},{3,4},{4,5},{5,6},{6,7},{7,8},{8,9},{9,10},{10,1... | collective-permute-start | bytes 3464 | tf_op jit(solution)/shard_map/ppermute | solution.py:496
  31.1 0.1 pad_add_fusion.1.par_ref
  31.2 0.7 collective-permute-done.prev_list
  31.9 0.0 collective-permute-done.1.near_ref
  31.9 0.0 collective-permute-done.2.far_ref
  31.9 29.9 %pairs.1 = (f32[49152,128]{1,0:T(8,128)S(1)}, f32[32768,128]{1,0:T(8,128)}, s32[4,65]{1,0:T(4,128)S(1)}) custom-call(s32[3]{0:T(128)S(1)} %pad_add_fusion.1.par_ref, s32[3,96]{1,0:T(4,128)S(1)} %pad_add_fusion.own_list, s32[3,96]{1,0:T(4,128)S(1)} %collective-permute-done.prev_list, f32[256,128]{1,0:T(8,128)S(1)} %tile_in.1.own_ref.inv_ref.refs_0_, ...), custom_call_target="tpu_custom_call" | custom-call | tf_op jit(solution)/shard_map/pairs/pallas_call | solution.py:519
  61.8 14.4 %apply.4.own_ref.refs_1_ = f32[96,128]{1,0:T(8,128)S(1)} custom-call(s32[3]{0:T(128)S(1)} %pad_add_fusion.1.par_ref, s32[4,65]{1,0:T(4,128)S(1)} %get-tuple-element.5.tab_ref, s32[3,96]{1,0:T(4,128)S(1)} %pad_add_fusion.own_list, s32[3,96]{1,0:T(4,128)S(1)} %collective-permute-done.prev_list, f32[49152,128]{1,0:T(8,128)S(1)} %get-tuple-element.6.tensor_ref, ...), custom_call_target="tpu_custom_call" | custom-call | tf_op jit(solution)/shard_map/apply/pallas_call | solution.py:541
  76.2 7.6 %collective-permute-start.3 = (f32[96,128]{1,0:T(8,128)S(1)}, f32[96,128]{1,0:T(8,128)S(1)}, u32[]{:S(2)}, u32[]{:S(2)}) collective-permute-start(f32[96,128]{1,0:T(8,128)S(1)} %apply.4.own_ref.refs_1_), channel_id=1, source_target_pairs={{0,1},{1,0},{2,3},{3,2},{4,5},{5,4},{6,7},{7,6},{8,9},{9,8},{10,11... | collective-permute-start | bytes 147464 | tf_op jit(solution)/shard_map/ppermute | solution.py:491
  83.8 0.0 collective-permute-start.4
  83.8 0.9 collective-permute-done.3.near_ref
  84.7 2.6 %collective-permute-done.4.far_ref = f32[96,128]{1,0:T(8,128)S(1)} collective-permute-done((f32[96,128]{1,0:T(8,128)S(1)}, f32[96,128]{1,0:T(8,128)S(1)}, u32[]{:S(2)}, u32[]{:S(2)}) %collective-permute-start.4) | collective-permute-done | bytes 49184 | tf_op jit(solution)/shard_map/ppermute | solution.py:491
  87.3 14.4 %apply.5.own_ref.refs_2_ = f32[96,128]{1,0:T(8,128)S(1)} custom-call(s32[3]{0:T(128)S(1)} %pad_add_fusion.1.par_ref, s32[4,65]{1,0:T(4,128)S(1)} %get-tuple-element.5.tab_ref, s32[3,96]{1,0:T(4,128)S(1)} %pad_add_fusion.own_list, s32[3,96]{1,0:T(4,128)S(1)} %collective-permute-done.prev_list, f32[49152,128]{1,0:T(8,128)S(1)} %get-tuple-element.6.tensor_ref, ...), custom_call_target="tpu_custom_call" | custom-call | tf_op jit(solution)/shard_map/apply/pallas_call | solution.py:541
  101.8 4.6 %collective-permute-start.5 = (f32[96,128]{1,0:T(8,128)S(1)}, f32[96,128]{1,0:T(8,128)S(1)}, u32[]{:S(2)}, u32[]{:S(2)}) collective-permute-start(f32[96,128]{1,0:T(8,128)S(1)} %apply.5.own_ref.refs_2_), channel_id=1, source_target_pairs={{0,1},{1,0},{2,3},{3,2},{4,5},{5,4},{6,7},{7,6},{8,9},{9,8},{10,11... | collective-permute-start | bytes 147464 | tf_op jit(solution)/shard_map/ppermute | solution.py:491
  106.4 0.0 collective-permute-start.6
  106.4 0.9 collective-permute-done.5.near_ref
  107.3 2.6 %collective-permute-done.6.far_ref = f32[96,128]{1,0:T(8,128)S(1)} collective-permute-done((f32[96,128]{1,0:T(8,128)S(1)}, f32[96,128]{1,0:T(8,128)S(1)}, u32[]{:S(2)}, u32[]{:S(2)}) %collective-permute-start.6) | collective-permute-done | bytes 49184 | tf_op jit(solution)/shard_map/ppermute | solution.py:491
  109.9 14.4 %apply.6.own_ref.refs_3_ = f32[96,128]{1,0:T(8,128)S(1)} custom-call(s32[3]{0:T(128)S(1)} %pad_add_fusion.1.par_ref, s32[4,65]{1,0:T(4,128)S(1)} %get-tuple-element.5.tab_ref, s32[3,96]{1,0:T(4,128)S(1)} %pad_add_fusion.own_list, s32[3,96]{1,0:T(4,128)S(1)} %collective-permute-done.prev_list, f32[49152,128]{1,0:T(8,128)S(1)} %get-tuple-element.6.tensor_ref, ...), custom_call_target="tpu_custom_call" | custom-call | tf_op jit(solution)/shard_map/apply/pallas_call | solution.py:541
  124.3 0.0 copy-start.1
  124.4 4.6 %collective-permute-start.7 = (f32[96,128]{1,0:T(8,128)S(1)}, f32[96,128]{1,0:T(8,128)S(1)}, u32[]{:S(2)}, u32[]{:S(2)}) collective-permute-start(f32[96,128]{1,0:T(8,128)S(1)} %apply.6.own_ref.refs_3_), channel_id=1, source_target_pairs={{0,1},{1,0},{2,3},{3,2},{4,5},{5,4},{6,7},{7,6},{8,9},{9,8},{10,11... | collective-permute-start | bytes 147464 | tf_op jit(solution)/shard_map/ppermute | solution.py:491
  129.0 0.0 collective-permute-start.8
  129.0 0.9 collective-permute-done.7.near_ref
  129.9 2.6 %collective-permute-done.8.far_ref = f32[96,128]{1,0:T(8,128)S(1)} collective-permute-done((f32[96,128]{1,0:T(8,128)S(1)}, f32[96,128]{1,0:T(8,128)S(1)}, u32[]{:S(2)}, u32[]{:S(2)}) %collective-permute-start.8) | collective-permute-done | bytes 49184 | tf_op jit(solution)/shard_map/ppermute | solution.py:491
  132.5 14.4 %apply.7.refs_4_ = f32[96,128]{1,0:T(8,128)S(1)} custom-call(s32[3]{0:T(128)S(1)} %pad_add_fusion.1.par_ref, s32[4,65]{1,0:T(4,128)S(1)} %get-tuple-element.5.tab_ref, s32[3,96]{1,0:T(4,128)S(1)} %pad_add_fusion.own_list, s32[3,96]{1,0:T(4,128)S(1)} %collective-permute-done.prev_list, f32[49152,128]{1,0:T(8,128)S(1)} %get-tuple-element.6.tensor_ref, ...), custom_call_target="tpu_custom_call" | custom-call | tf_op jit(solution)/shard_map/apply/pallas_call | solution.py:541
  146.9 0.1 gram.1
  147.1 0.7 broadcast_in_dim.2
  147.7 11.7 %all-to-all-start = ((f32[128,1,128]{2,1,0:T(1,128)}), f32[128,1,128]{2,1,0:T(1,128)S(1)}, u32[]{:S(2)}, u32[]{:S(2)}) async-start(f32[128,1,128]{2,1,0:T(1,128)} %broadcast_in_dim.2), calls=%async_computation | async-start | bytes 131072 | tf_op jit(solution)/shard_map/all_to_all | solution.py:573
  159.4 0.0 copy-done.1
  159.4 0.8 inverse.1.inv_ref
  160.3 11.4 %all-to-all-done = f32[128,1,128]{2,1,0:T(1,128)S(1)} async-done(((f32[128,1,128]{2,1,0:T(1,128)}), f32[128,1,128]{2,1,0:T(1,128)S(1)}, u32[]{:S(2)}, u32[]{:S(2)}) %all-to-all-start) | async-done | bytes 65568 | tf_op jit(solution)/shard_map/all_to_all | solution.py:573
  171.7 4.0 %outputs.1 = (f32[3,4096]{1,0:T(4,128)}, f32[3,4096]{1,0:T(4,128)}) custom-call(f32[128,128]{1,0:T(8,128)S(1)} %bitcast.7, s32[32,128]{1,0:T(8,128)S(1)} %inverse.1.inv_ref, f32[256,128]{1,0:T(8,128)S(1)} %tile_in.1.own_ref.inv_ref.refs_0_, f32[96,128]{1,0:T(8,128)S(1)} %apply.4.own_ref.refs_1_, f32[96,128]{1,0:T(8,128)S(1)} %apply.5.own_ref.refs_2_, ...), custom_call_target="tpu_custom_call" | custom-call | tf_op jit(solution)/shard_map/outputs/pallas_call | solution.py:574
  (1 shorter events, 0.0 us)
Async XLA Ops:
  0.6 0.7 copy-start
  1.4 0.8 copy-start.2
  2.2 0.8 copy-start.3
  3.0 0.7 copy-start.4
  7.0 24.9 %collective-permute-start.1 = (f32[256,128]{1,0:T(8,128)S(1)}, f32[256,128]{1,0:T(8,128)S(1)}, u32[]{:S(2)}, u32[]{:S(2)}) collective-permute-start(f32[256,128]{1,0:T(8,128)S(1)} %tile_in.1.own_ref.inv_ref.refs_0_), channel_id=1, source_target_pairs={{0,1},{1,0},{2,3},{3,2},{4,5},{5,4},{6,7},{7,6},{8,9},{9,8},{10,11... | collective-permute-start | bytes 393224 | tf_op jit(solution)/shard_map/ppermute | solution.py:491
  27.5 4.4 %collective-permute-start.2 = (f32[256,128]{1,0:T(8,128)S(1)}, f32[256,128]{1,0:T(8,128)S(1)}, u32[]{:S(2)}, u32[]{:S(2)}) collective-permute-start(f32[256,128]{1,0:T(8,128)S(1)} %tile_in.1.own_ref.inv_ref.refs_0_), channel_id=1, source_target_pairs={{0,127},{1,2},{2,1},{3,4},{4,3},{5,6},{6,5},{7,8},{8,7},{9,10},{10... | collective-permute-start | bytes 393224 | tf_op jit(solution)/shard_map/ppermute | solution.py:491
  29.3 2.6 %collective-permute-start = (s32[3,96]{1,0:T(4,128)S(1)}, s32[3,96]{1,0:T(4,128)S(1)}, u32[]{:S(2)}, u32[]{:S(2)}) collective-permute-start(s32[3,96]{1,0:T(4,128)S(1)} %pad_add_fusion.own_list), channel_id=1, source_target_pairs={{0,1},{1,2},{2,3},{3,4},{4,5},{5,6},{6,7},{7,8},{8,9},{9,10},{10,1... | collective-permute-start | bytes 3464 | tf_op jit(solution)/shard_map/ppermute | solution.py:496
  76.2 8.5 %collective-permute-start.3 = (f32[96,128]{1,0:T(8,128)S(1)}, f32[96,128]{1,0:T(8,128)S(1)}, u32[]{:S(2)}, u32[]{:S(2)}) collective-permute-start(f32[96,128]{1,0:T(8,128)S(1)} %apply.4.own_ref.refs_1_), channel_id=1, source_target_pairs={{0,1},{1,0},{2,3},{3,2},{4,5},{5,4},{6,7},{7,6},{8,9},{9,8},{10,11... | collective-permute-start | bytes 147464 | tf_op jit(solution)/shard_map/ppermute | solution.py:491
  83.8 3.5 %collective-permute-start.4 = (f32[96,128]{1,0:T(8,128)S(1)}, f32[96,128]{1,0:T(8,128)S(1)}, u32[]{:S(2)}, u32[]{:S(2)}) collective-permute-start(f32[96,128]{1,0:T(8,128)S(1)} %apply.4.own_ref.refs_1_), channel_id=1, source_target_pairs={{0,127},{1,2},{2,1},{3,4},{4,3},{5,6},{6,5},{7,8},{8,7},{9,10},{10... | collective-permute-start | bytes 147464 | tf_op jit(solution)/shard_map/ppermute | solution.py:491
  101.8 5.5 %collective-permute-start.5 = (f32[96,128]{1,0:T(8,128)S(1)}, f32[96,128]{1,0:T(8,128)S(1)}, u32[]{:S(2)}, u32[]{:S(2)}) collective-permute-start(f32[96,128]{1,0:T(8,128)S(1)} %apply.5.own_ref.refs_2_), channel_id=1, source_target_pairs={{0,1},{1,0},{2,3},{3,2},{4,5},{5,4},{6,7},{7,6},{8,9},{9,8},{10,11... | collective-permute-start | bytes 147464 | tf_op jit(solution)/shard_map/ppermute | solution.py:491
  106.4 3.5 %collective-permute-start.6 = (f32[96,128]{1,0:T(8,128)S(1)}, f32[96,128]{1,0:T(8,128)S(1)}, u32[]{:S(2)}, u32[]{:S(2)}) collective-permute-start(f32[96,128]{1,0:T(8,128)S(1)} %apply.5.own_ref.refs_2_), channel_id=1, source_target_pairs={{0,127},{1,2},{2,1},{3,4},{4,3},{5,6},{6,5},{7,8},{8,7},{9,10},{10... | collective-permute-start | bytes 147464 | tf_op jit(solution)/shard_map/ppermute | solution.py:491
  124.3 35.1 %copy-start.1 = (s32[4096]{0:T(1024)S(1)}, s32[4096]{0:T(1024)}, u32[]{:S(2)}) copy-start(s32[4096]{0:T(1024)} %param.9) | copy-start | bytes 49156
  124.4 5.5 %collective-permute-start.7 = (f32[96,128]{1,0:T(8,128)S(1)}, f32[96,128]{1,0:T(8,128)S(1)}, u32[]{:S(2)}, u32[]{:S(2)}) collective-permute-start(f32[96,128]{1,0:T(8,128)S(1)} %apply.6.own_ref.refs_3_), channel_id=1, source_target_pairs={{0,1},{1,0},{2,3},{3,2},{4,5},{5,4},{6,7},{7,6},{8,9},{9,8},{10,11... | collective-permute-start | bytes 147464 | tf_op jit(solution)/shard_map/ppermute | solution.py:491
  129.0 3.5 %collective-permute-start.8 = (f32[96,128]{1,0:T(8,128)S(1)}, f32[96,128]{1,0:T(8,128)S(1)}, u32[]{:S(2)}, u32[]{:S(2)}) collective-permute-start(f32[96,128]{1,0:T(8,128)S(1)} %apply.6.own_ref.refs_3_), channel_id=1, source_target_pairs={{0,127},{1,2},{2,1},{3,4},{4,3},{5,6},{6,5},{7,8},{8,7},{9,10},{10... | collective-permute-start | bytes 147464 | tf_op jit(solution)/shard_map/ppermute | solution.py:491
  147.7 23.9 %all-to-all-start = ((f32[128,1,128]{2,1,0:T(1,128)}), f32[128,1,128]{2,1,0:T(1,128)S(1)}, u32[]{:S(2)}, u32[]{:S(2)}) async-start(f32[128,1,128]{2,1,0:T(1,128)} %broadcast_in_dim.2), calls=%async_computation | async-start | bytes 131072 | tf_op jit(solution)/shard_map/all_to_all | solution.py:573

commit v2 on v1

v2 whole, which is shorter than its diff:
```python
import functools

import jax
import jax.numpy as jnp
from jax import lax
from jax.experimental import pallas as pl
from jax.experimental.pallas import tpu as pltpu
from jax.sharding import PartitionSpec as P

ITERS = 4
REP_GX = ("rep", "gx")
THOLE = 0.39
SHIFT = 2.5
SCALE = 1.5
MATS = 4
OUT_SLOTS = 8
SLOTS = 10
MIB = 2**20

F32 = jnp.float32
VMEM = pl.BlockSpec(memory_space=pltpu.VMEM)
SMEM = pl.BlockSpec(memory_space=pltpu.SMEM)
HBM = pl.BlockSpec(memory_space=pltpu.MemorySpace.HBM)


def spread(row, height=8):
    return jnp.broadcast_to(row, (height, row.shape[1]))


def lane_pick(row_block, lanes):
    return jnp.take_along_axis(row_block, lanes, axis=1)


def params(mib):
    return pltpu.CompilerParams(vmem_limit_bytes=mib * MIB)


def tile_in_kernel(pos_hbm, pol_hbm, fld_hbm, idx_hbm, out_ref, pos_ref, pol_ref, fld_ref, idx_ref, sems):
    copies = [
        pltpu.make_async_copy(source, target, sems.at[k])
        for k, (source, target) in enumerate(
            ((idx_hbm, idx_ref), (pos_hbm, pos_ref), (pol_hbm, pol_ref), (fld_hbm, fld_ref))
        )
    ]
    for copy in copies:
        copy.start()
    for copy in copies:
        copy.wait()
    tiles, width = idx_ref.shape
    for q in range(tiles // 8):
        rows = idx_ref[8 * q : 8 * q + 8, :]
        high = rows // width
        low = rows - high * width

        def step(h, acc):
            at = pl.ds(pl.multiple_of(h * width, width), width)
            hit = high == h
            new = []
            for c in range(7):
                if c < 3:
                    row = pos_ref[c : c + 1, at]
                elif c == 3:
                    row = pol_ref[0:1, at]
                else:
                    row = fld_ref[c - 4 : c - 3, at]
                new.append(jnp.where(hit, lane_pick(spread(row), low), acc[c]))
            return tuple(new)

        acc = lax.fori_loop(0, tiles, step, (jnp.zeros((8, width), F32),) * 7, unroll=16)
        values = list(acc[:3]) + [lax.rsqrt(acc[3])] + list(acc[4:]) + [1.0 / acc[3]]
        for c in range(8):
            out_ref[c * tiles + 8 * q : c * tiles + 8 * q + 8, :] = values[c]


def inverse_kernel(idx_ref, out_ref):
    tiles, width = idx_ref.shape
    total = jnp.zeros((2 * tiles, width), F32)
    lane = lax.broadcasted_iota(jnp.int32, (tiles, width), 1).astype(F32)
    row_id = lax.broadcasted_iota(jnp.int32, (tiles, width), 0)
    low_id = lax.broadcasted_iota(jnp.int32, (width, width), 0)
    for t in range(tiles):
        row = idx_ref[t : t + 1, :]
        high = row // width
        low = row - high * width
        hit = spread(high, tiles) == row_id
        left = jnp.concatenate([jnp.where(hit, float(t), 0.0), jnp.where(hit, lane, 0.0)], axis=0)
        right = jnp.where(spread(low, width) == low_id, 1.0, 0.0)
        total = total + lax.dot_general(
            left.astype(jnp.bfloat16),
            right.astype(jnp.bfloat16),
            (((1,), (1,)), ((), ())),
            preferred_element_type=F32,
        )
    out_ref[...] = (total[:tiles] * float(width) + total[tiles:] + 0.5).astype(jnp.int32)


def take_neighbours(par, near_ref, far_ref, nb_ref, start, rows):
    nb_ref[pl.ds(pl.multiple_of(par * rows, 8), rows), :] = near_ref[start : start + rows, :]
    nb_ref[pl.ds(pl.multiple_of((1 - par) * rows, 8), rows), :] = far_ref[start : start + rows, :]


def pair_coefficients(off, ci, rj, same):
    dist_sq = off[0] * off[0] + off[1] * off[1] + off[2] * off[2]
    if same is not None:
        dist_sq = jnp.where(same, 1.0, dist_sq)
    inv = lax.rsqrt(dist_sq)
    damp = (dist_sq * (dist_sq * inv)) * (ci * rj)
    decay = jnp.exp(-damp)
    inv_sq = inv * inv
    cube = inv_sq * inv
    g3 = (1.0 - decay) * cube
    g5 = (3.0 - (3.0 + 3.0 * damp) * decay) * (cube * inv_sq)
    root = g5 * lax.rsqrt(g5)
    if same is not None:
        g3 = jnp.where(same, 0.0, g3)
        root = jnp.where(same, 0.0, root)
    return [root * off[0], root * off[1], root * off[2], g3]


def pack_job(t, n, slot, y, z, spare=0):
    return t + n * 256 + slot * 65536 + (y + 2 * z + 4 * spare) * 16777216


def read_job(tab_ref, group, at, tiles):
    word = tab_ref[1 + group, at]
    t = word & 255
    last = word >> 24
    return t, (word >> 8) & 255, (word >> 16) & 255, t + (last >> 2) * tiles, last & 1, (last >> 1) & 1


def row_block(ref, first, tiles, n, count):
    return [spread(ref[pl.ds(first + c * tiles + n, 1), :]) for c in range(count)]


def write_columns(col_ref, place, own_ref, tiles, t):
    width = own_ref.shape[1]
    for c in range(4):
        row = own_ref[pl.ds(c * tiles + t, 1), :]
        if c == 3:
            row = row * THOLE
        first = (place * 4 + c) * width
        col_ref[first : first + width, :] = spread(row, width).T


def pair_block(col_ref, place, row, store, same, lead):
    width = col_ref.shape[1]
    for k in range(width // 8):
        first = place * 4 * width + 8 * k
        col = [col_ref[first + c * width : first + c * width + 8, :] for c in range(4)]
        if lead is not None:
            off = [(col[c] + lead[c]) - row[c] for c in range(3)]
        else:
            off = [row[c] - col[c] for c in range(3)]
        mask = None
        if same:
            i = lax.broadcasted_iota(jnp.int32, (8, width), 0) + 8 * k
            j = lax.broadcasted_iota(jnp.int32, (8, width), 1)
            mask = i == j
        store(k, pair_coefficients(off, col[3], row[3], mask))


def store_at(ref, base):
    width = ref.shape[1]

    def store(k, mats):
        for m in range(MATS):
            ref[pl.ds(base + m * width + 8 * k, 8), :] = mats[m]

    return store


def halves(count):
    return (count + 1) // 2


def local_pairs_kernel(own_list, own_shift, own_ref, tensor_ref, tab_ref, col_ref, *, boxes):
    tiles = own_ref.shape[0] // 8
    width = own_ref.shape[1]
    extra = own_list.shape[0] - 1
    cap = extra * tiles
    size = MATS * width

    def sort(k, counts):
        inner, outer = counts
        e = k // tiles
        t = k - e * tiles
        n = own_list[1 + e, t]
        y = own_shift[1 + e, 0, t]
        z = own_shift[1 + e, 1, t]
        near = (n < tiles).astype(jnp.int32)
        tab_ref[1, inner] = pack_job(t, n, tiles + k, y, z)
        tab_ref[2, outer] = pack_job(t, n - tiles * (1 - near), tiles + k, y, z)
        return inner + near, outer + 1 - near

    inner, outer = lax.fori_loop(0, cap, sort, (jnp.int32(0), jnp.int32(0)), unroll=8)
    tab_ref[1, inner] = pack_job(0, 0, tiles + cap, 1, 1, 1)
    tab_ref[2, outer] = pack_job(0, 0, tiles + cap, 1, 1, 1)
    tab_ref[0, 0] = inner
    tab_ref[0, 1] = outer

    def self_job(i, _):
        for p in range(2):
            t = 2 * i + p
            write_columns(col_ref, p, own_ref, tiles, t)
            store = store_at(tensor_ref, pl.multiple_of(t * size, size))
            pair_block(col_ref, p, row_block(own_ref, 0, tiles, t, 4), store, True, None)
        return 0

    lax.fori_loop(0, tiles // 2, self_job, 0)

    def inner_job(i, _):
        for p in range(2):
            t, n, slot, _tw, y, z = read_job(tab_ref, 0, 2 * i + p, tiles)
            write_columns(col_ref, p, own_ref, tiles, t)
            row = row_block(own_ref, 0, tiles, n, 4)
            row = [row[0], row[1] + y.astype(F32) * boxes[1], row[2] + z.astype(F32) * boxes[2], row[3]]
            pair_block(col_ref, p, row, store_at(tensor_ref, pl.multiple_of(slot * size, size)), False, None)
        return 0

    lax.fori_loop(0, halves(inner), inner_job, 0)


def cross_pairs_kernel(
    par_ref, own_tab, prev_list, prev_shift, own_ref, near_ref, far_ref, tensor_in,
    tensor_ref, prev_hbm, tab_ref, nb_ref, col_ref, out_slots, sems,
    *, boxes,
):
    del tensor_in
    tiles = own_ref.shape[0] // 8
    width = own_ref.shape[1]
    extra = prev_list.shape[0] - 1
    cap = extra * tiles
    size = MATS * width
    rows = 4 * tiles
    par = par_ref[0]
    wrap_next = par_ref[1].astype(F32) * boxes[0]
    wrap_prev = par_ref[2].astype(F32) * boxes[0]
    take_neighbours(par, near_ref, far_ref, nb_ref, 0, rows)

    def sort(k, count):
        e = k // tiles
        t = k - e * tiles
        n = prev_list[1 + e, t]
        own = jnp.maximum(n - tiles, 0)
        tab_ref[1, count] = pack_job(own, t, 0, prev_shift[1 + e, 0, t], prev_shift[1 + e, 1, t])
        return count + (n >= tiles).astype(jnp.int32)

    behind = lax.fori_loop(0, cap, sort, jnp.int32(0), unroll=8)
    tab_ref[1, behind] = pack_job(0, 0, 0, 0, 0, 1)
    tab_ref[0, 0] = behind
    outer = own_tab[0, 1]

    def out_copy(i):
        slot = lax.rem(i, OUT_SLOTS)
        return pltpu.make_async_copy(
            out_slots.at[pl.ds(pl.multiple_of(slot * size, size), size), :],
            prev_hbm.at[pl.ds(pl.multiple_of(i * size, size), size), :],
            sems.at[slot],
        )

    def behind_job(i, _):
        jobs = [read_job(tab_ref, 0, 2 * i + p, tiles) for p in range(2)]
        for p in range(2):

            @pl.when(2 * i + p >= OUT_SLOTS)
            def _():
                out_copy(2 * i + p - OUT_SLOTS).wait()

        for p in range(2):
            t, n, _slot, _tw, y, z = jobs[p]
            write_columns(col_ref, p, own_ref, tiles, t)
            lead = (wrap_prev, y.astype(F32) * boxes[1], z.astype(F32) * boxes[2])
            base = pl.multiple_of(lax.rem(2 * i + p, OUT_SLOTS) * size, size)
            pair_block(col_ref, p, row_block(nb_ref, rows, tiles, n, 4), store_at(out_slots, base), False, lead)
        for p in range(2):
            out_copy(2 * i + p).start()
        return 0

    steps = halves(behind)
    lax.fori_loop(0, steps, behind_job, 0)

    def outer_job(i, _):
        for p in range(2):
            t, n, slot, _tw, y, z = read_job(own_tab, 1, 2 * i + p, tiles)
            write_columns(col_ref, p, own_ref, tiles, t)
            row = row_block(nb_ref, 0, tiles, n, 4)
            row = [
                row[0] + wrap_next, row[1] + y.astype(F32) * boxes[1], row[2] + z.astype(F32) * boxes[2], row[3]
            ]
            pair_block(col_ref, p, row, store_at(tensor_ref, pl.multiple_of(slot * size, size)), False, None)
        return 0

    lax.fori_loop(0, halves(outer), outer_job, 0)

    def drain(i, _):
        out_copy(i).wait()
        return 0

    lax.fori_loop(jnp.maximum(2 * steps - OUT_SLOTS, 0), 2 * steps, drain, 0)


def left_at(tile, c, k, width):
    return pl.ds(pl.multiple_of((tile * 3 + c) * width, width) + 8 * k, 8)


def one_side(left_ref, source, base, tile, row, fresh):
    width = source.shape[1]
    for k in range(width // 8):
        s = [source[pl.ds(base + m * width + 8 * k, 8), :] for m in range(MATS)]
        lift = s[0] * row[0] + s[1] * row[1] + s[2] * row[2]
        for c in range(3):
            at = left_at(tile, c, k, width)
            value = s[c] * lift - s[3] * row[c]
            left_ref[at, :] = value if fresh else left_ref[at, :] + value


def lane_total(left_ref, t, c, width):
    block = left_ref[pl.ds(pl.multiple_of((t * 3 + c) * width, width), width), :].T
    return jnp.sum(block, axis=0, keepdims=True)


def local_apply_kernel(tab_ref, tensor_ref, own_ref, out_ref, left_ref, right_ref, *, start):
    width = own_ref.shape[1]
    rows = out_ref.shape[0]
    tiles = rows // 3
    size = MATS * width
    right_ref[...] = jnp.zeros_like(right_ref)

    def self_job(i, _):
        for p in range(2):
            t = 2 * i + p
            row = row_block(own_ref, start, tiles, t, 3)
            one_side(left_ref, tensor_ref, pl.multiple_of(t * size, size), t, row, True)
        return 0

    lax.fori_loop(0, tiles // 2, self_job, 0)
    first = pl.multiple_of(tiles * 3 * width, width)
    left_ref[pl.ds(first, 3 * width), :] = jnp.zeros((3 * width, width), F32)

    def inner_job(i, _):
        jobs = [read_job(tab_ref, 0, 2 * i + p, tiles)[:4] for p in range(2)]
        cols = [
            [spread(own_ref[pl.ds(start + c * tiles + job[0], 1), :], width).T for c in range(3)] for job in jobs
        ]
        for (t, n, slot, tw), col in zip(jobs, cols):
            row = row_block(own_ref, start, tiles, n, 3)
            one_side(left_ref, tensor_ref, pl.multiple_of(slot * size, size), tw, row, False)
        for (t, n, slot, tw), col in zip(jobs, cols):
            base = pl.multiple_of(slot * size, size)
            target = jnp.where(tw < tiles, n, tiles)
            places = [pl.ds(pl.multiple_of((target * 3 + c) * 8, 8), 8) for c in range(3)]
            acc = [jnp.zeros((8, width), F32)] * 3
            for q in range(width // 8):
                s = [tensor_ref[pl.ds(base + m * width + 8 * q, 8), :] for m in range(MATS)]
                mine = [col[c][8 * q : 8 * q + 8, :] for c in range(3)]
                lift = s[0] * mine[0] + s[1] * mine[1] + s[2] * mine[2]
                for c in range(3):
                    acc[c] = acc[c] + (s[c] * lift - s[3] * mine[c])
            for c in range(3):
                right_ref[places[c], :] = right_ref[places[c], :] + acc[c]
        return 0

    lax.fori_loop(0, halves(tab_ref[0, 0]), inner_job, 0)

    def finish(t, _):
        for c in range(3):
            field = lane_total(left_ref, t, c, width) + jnp.sum(
                right_ref[pl.ds(pl.multiple_of((t * 3 + c) * 8, 8), 8), :], axis=0, keepdims=True
            )
            out_ref[pl.ds(c * tiles + t, 1), :] = field
        return 0

    lax.fori_loop(0, tiles, finish, 0, unroll=4)


def cross_apply_kernel(
    par_ref, own_tab, prev_tab, tensor_ref, prev_hbm, own_ref, near_ref, far_ref, inv_ref, part_ref,
    out_ref, nb_ref, left_ref, slots_ref, sems,
    *, start, inv_start,
):
    width = own_ref.shape[1]
    rows = out_ref.shape[0]
    tiles = rows // 3
    size = MATS * width
    behind = prev_tab[0, 0]

    def in_copy(i):
        slot = lax.rem(i, SLOTS)
        return pltpu.make_async_copy(
            prev_hbm.at[pl.ds(pl.multiple_of(i * size, size), size), :],
            slots_ref.at[pl.ds(pl.multiple_of(slot * size, size), size), :],
            sems.at[slot],
        )

    steps = halves(behind)

    def begin(i, _):
        in_copy(i).start()
        return 0

    lax.fori_loop(0, jnp.minimum(2 * steps, SLOTS), begin, 0)
    take_neighbours(par_ref[0], near_ref, far_ref, nb_ref, start, rows)

    def clear(i, _):
        left_ref[pl.ds(pl.multiple_of(i * width, width), width), :] = jnp.zeros((width, width), F32)
        return 0

    lax.fori_loop(0, rows + 3, clear, 0, unroll=3)

    def outer_job(i, _):
        for p in range(2):
            t, n, slot, tw = read_job(own_tab, 1, 2 * i + p, tiles)[:4]
            row = row_block(nb_ref, 0, tiles, n, 3)
            one_side(left_ref, tensor_ref, pl.multiple_of(slot * size, size), tw, row, False)
        return 0

    lax.fori_loop(0, halves(own_tab[0, 1]), outer_job, 0)

    def behind_job(i, _):
        jobs = [read_job(prev_tab, 0, 2 * i + p, tiles)[:4] for p in range(2)]
        for p in range(2):
            in_copy(2 * i + p).wait()
        for p in range(2):
            t, n, slot, tw = jobs[p]
            base = pl.multiple_of(lax.rem(2 * i + p, SLOTS) * size, size)
            one_side(left_ref, slots_ref, base, tw, row_block(nb_ref, rows, tiles, n, 3), False)

        @pl.when(2 * i + SLOTS < 2 * steps)
        def _():
            for p in range(2):
                in_copy(2 * i + p + SLOTS).start()

        return 0

    lax.fori_loop(0, steps, behind_job, 0)

    def finish(t, _):
        weight = (inv_ref[pl.ds(inv_start + t, 1), :] - SHIFT) * (1.0 / SCALE)
        for c in range(3):
            at = pl.ds(c * tiles + t, 1)
            field = lane_total(left_ref, t, c, width) + part_ref[at, :]
            mine = own_ref[pl.ds(start + c * tiles + t, 1), :]
            out_ref[at, :] = mine * weight - field * (1.0 / SCALE)
        return 0

    lax.fori_loop(0, tiles, finish, 0, unroll=4)


PAIRS = [(i, j) for i in range(ITERS + 1) for j in range(i, ITERS + 1)]


def gram_kernel(*refs, start):
    vectors, out_ref = refs[:-1], refs[-1]
    rows, width = vectors[-1].shape
    lane = lax.broadcasted_iota(jnp.int32, (1, width), 1)
    total = jnp.zeros((1, width), F32)
    starts = (start,) + (0,) * ITERS
    for n, (i, j) in enumerate(PAIRS):
        product = vectors[i][starts[i] : starts[i] + rows, :] * vectors[j][starts[j] : starts[j] + rows, :]
        line = jnp.sum(product, axis=0, keepdims=True)
        total = jnp.where(lane == n, jnp.sum(line, axis=1, keepdims=True), total)
    out_ref[...] = total


def untile_kernel(inv_ref, *refs, start):
    vectors, outs = refs[: ITERS + 1], refs[ITERS + 1 :]
    tiles, width = inv_ref.shape
    starts = (start,) + (0,) * ITERS
    zero = jnp.zeros((8, width), F32)
    for q in range(tiles // 8):
        index = inv_ref[8 * q : 8 * q + 8, :]
        high = index // width
        low = index - high * width

        def step(h, acc):
            hit = high == h
            return tuple(
                jnp.where(hit, lane_pick(spread(vectors[n // 3][pl.ds(starts[n // 3] + n % 3 * tiles + h, 1), :]), low), acc[n])
                for n in range(3 * (ITERS + 1))
            )

        acc = lax.fori_loop(0, tiles, step, (zero,) * (3 * (ITERS + 1)), unroll=8)
        for n in range(3 * (ITERS + 1)):
            for s in range(8):
                at = (8 * q + s) * width
                outs[n // 3][n % 3 : n % 3 + 1, at : at + width] = acc[n][s : s + 1, :]


def output_kernel(parts_ref, *refs):
    vectors, (dip_ref, res_ref) = refs[: ITERS + 1], refs[ITERS + 1 :]
    width = parts_ref.shape[1]
    sums = jnp.sum(parts_ref[...], axis=0, keepdims=True)
    lane = lax.broadcasted_iota(jnp.int32, (1, width), 1)
    gram = {}
    for n, (i, j) in enumerate(PAIRS):
        value = jnp.sum(jnp.where(lane == n, sums, 0.0), axis=1, keepdims=True)
        gram[i, j] = gram[j, i] = jnp.broadcast_to(value, (1, width))

    def add(a, b):
        return b if a is None else a if b is None else a + b

    def inner(a, b):
        total = None
        for i in range(ITERS + 1):
            line = None
            for j in range(ITERS + 1):
                if a[i] is not None and b[j] is not None:
                    line = add(line, b[j] * gram[i, j])
            if line is not None:
                total = add(total, a[i] * line)
        return total

    def operate(a):
        out = [None if v is None else SHIFT * v for v in a]
        for i in range(ITERS):
            if a[i] is not None:
                out[i + 1] = add(out[i + 1], SCALE * a[i])
        return out

    x = [None] * (ITERS + 1)
    r = [jnp.ones((1, width), F32)] + [None] * ITERS
    d = list(r)
    norm = inner(r, r)
    for step in range(ITERS):
        q = operate(d)
        size = norm / inner(d, q)
        x = [add(x[k], None if d[k] is None else size * d[k]) for k in range(ITERS + 1)]
        r = [add(r[k], None if q[k] is None else -size * q[k]) for k in range(ITERS + 1)]
        if step + 1 < ITERS:
            new = inner(r, r)
            ratio = new / norm
            d = [add(r[k], None if d[k] is None else ratio * d[k]) for k in range(ITERS + 1)]
            norm = new
    x = [None if v is None else jnp.broadcast_to(v, (3, width)) for v in x]
    r = [jnp.broadcast_to(v, (3, width)) for v in r]
    for b in range(dip_ref.shape[1] // width):
        at = slice(b * width, (b + 1) * width)
        values = [vectors[k][:, at] for k in range(ITERS + 1)]
        for out, weights in ((dip_ref, x), (res_ref, r)):
            total = None
            for k in range(ITERS + 1):
                if weights[k] is not None:
                    total = add(total, weights[k] * values[k])
            out[:, at] = total


def shape(rows, width, dtype=F32):
    return jax.ShapeDtypeStruct((rows, width), dtype)


def cost(flops):
    return pl.CostEstimate(flops=flops, bytes_accessed=1_000_000, transcendentals=0)


def on_device(positions, polar, field_ext, tile_atom, tile_list, image_shift):
    tiles, links = tile_list.shape
    atoms = tile_atom.shape[0]
    width = atoms // tiles
    slabs = lax.axis_size("gx")
    slab = lax.axis_index("gx")
    rows = 3 * tiles
    cap = tiles * (links - 1)
    size = MATS * width
    boxes = (4.0 * slabs, 128.0, 2.0 * tiles)
    near_pairs = [(i, i ^ 1) for i in range(slabs)]
    far_pairs = [(i, ((i + 1) ^ 1) - 1 if 0 < i < slabs - 1 else slabs - 1 - i) for i in range(slabs)]
    ahead = [(i, (i + 1) % slabs) for i in range(slabs)]

    def swap(value):
        return lax.ppermute(value, "gx", far_pairs), lax.ppermute(value, "gx", near_pairs)

    own_list = tile_list.T
    own_shift = image_shift.transpose(2, 0, 1)
    prev_list = lax.ppermute(own_list, "gx", ahead)
    prev_shift = lax.ppermute(own_shift, "gx", ahead)
    par = jnp.stack([slab % 2, (slab == slabs - 1).astype(jnp.int32), (slab == 0).astype(jnp.int32)])
    par = par.astype(jnp.int32)
    index = tile_atom.reshape(tiles, width)
    packed = pl.pallas_call(
        tile_in_kernel,
        out_shape=shape(8 * tiles, width),
        in_specs=[HBM] * 4,
        out_specs=VMEM,
        scratch_shapes=[
            pltpu.VMEM((3, atoms), F32),
            pltpu.VMEM((1, atoms), F32),
            pltpu.VMEM((3, atoms), F32),
            pltpu.VMEM((tiles, width), jnp.int32),
            pltpu.SemaphoreType.DMA((4,)),
        ],
        compiler_params=params(4),
        name="tile_in",
    )(*(pltpu.with_memory_space_constraint(v, pltpu.MemorySpace.HBM) for v in (positions, polar.reshape(1, -1), field_ext, index)))
    far, near = swap(packed)
    inverse = pl.pallas_call(
        inverse_kernel,
        out_shape=shape(tiles, width, jnp.int32),
        in_specs=[VMEM],
        out_specs=VMEM,
        compiler_params=params(4),
        cost_estimate=cost(4_000_000),
        name="inverse",
    )(index)
    table = shape(3, cap + 1, jnp.int32)
    tensor_shape = pltpu.VMEM(((tiles + cap + 1) * size, width), F32)
    col_shape = pltpu.VMEM((2 * 4 * width, width), F32)
    tensor, own_tab = pl.pallas_call(
        functools.partial(local_pairs_kernel, boxes=boxes),
        out_shape=(tensor_shape, table),
        in_specs=[SMEM, SMEM, VMEM],
        out_specs=(VMEM, SMEM),
        scratch_shapes=[col_shape],
        compiler_params=params(4),
        cost_estimate=cost(60_000_000),
        name="local_pairs",
    )(own_list, own_shift, packed)
    tensor, prev_tensor, prev_tab = pl.pallas_call(
        functools.partial(cross_pairs_kernel, boxes=boxes),
        out_shape=(
            tensor_shape,
            pltpu.MemorySpace.HBM(((cap + 1) * size, width), F32),
            table,
        ),
        in_specs=[SMEM] * 4 + [VMEM] * 4,
        out_specs=(VMEM, HBM, SMEM),
        scratch_shapes=[
            pltpu.VMEM((2 * 4 * tiles, width), F32),
            col_shape,
            pltpu.VMEM((OUT_SLOTS * size, width), F32),
            pltpu.SemaphoreType.DMA((OUT_SLOTS,)),
        ],
        input_output_aliases={7: 0},
        compiler_params=params(6),
        cost_estimate=cost(60_000_000),
        name="cross_pairs",
    )(par, own_tab, prev_list, prev_shift, packed, near, far, tensor)
    prev_tensor = pltpu.with_memory_space_constraint(prev_tensor, pltpu.MemorySpace.HBM)
    left_shape = pltpu.VMEM(((rows + 3) * width, width), F32)

    def apply(vector, near, far, start):
        part = pl.pallas_call(
            functools.partial(local_apply_kernel, start=start),
            out_shape=shape(rows, width),
            in_specs=[SMEM, VMEM, VMEM],
            out_specs=VMEM,
            scratch_shapes=[left_shape, pltpu.VMEM((8 * (rows + 3), width), F32)],
            compiler_params=params(9),
            cost_estimate=cost(60_000_000),
            name="local_apply",
        )(own_tab, tensor, vector)
        return pl.pallas_call(
            functools.partial(cross_apply_kernel, start=start, inv_start=7 * tiles),
            out_shape=shape(rows, width),
            in_specs=[SMEM] * 3 + [VMEM, HBM] + [VMEM] * 5,
            out_specs=VMEM,
            scratch_shapes=[
                pltpu.VMEM((2 * rows, width), F32),
                left_shape,
                pltpu.VMEM((SLOTS * size, width), F32),
                pltpu.SemaphoreType.DMA((SLOTS,)),
            ],
            compiler_params=params(10),
            cost_estimate=cost(60_000_000),
            name="cross_apply",
        )(par, own_tab, prev_tab, tensor, prev_tensor, vector, near, far, packed, part)

    start = 4 * tiles
    basis = [packed]
    vector = apply(packed, near, far, start)
    basis.append(vector)
    for _ in range(ITERS - 1):
        far, near = swap(vector)
        vector = apply(vector, near, far, 0)
        basis.append(vector)
    gram = pl.pallas_call(
        functools.partial(gram_kernel, start=start),
        out_shape=shape(1, width),
        in_specs=[VMEM] * (ITERS + 1),
        out_specs=VMEM,
        compiler_params=params(4),
        name="gram",
    )(*basis)
    parts = lax.all_to_all(jnp.broadcast_to(gram, (slabs, width)), "gx", 0, 0, tiled=True)
    natural = pl.pallas_call(
        functools.partial(untile_kernel, start=start),
        out_shape=(shape(3, atoms),) * (ITERS + 1),
        in_specs=[VMEM] * (ITERS + 2),
        out_specs=(VMEM,) * (ITERS + 1),
        compiler_params=params(4),
        cost_estimate=cost(60_000_000),
        name="untile",
    )(inverse, *basis)
    return pl.pallas_call(
        output_kernel,
        out_shape=(shape(3, atoms), shape(3, atoms)),
        in_specs=[VMEM] * (ITERS + 2),
        out_specs=(VMEM, VMEM),
        compiler_params=params(4),
        name="outputs",
    )(parts, *natural)


def solution(mesh):
    return jax.shard_map(
        on_device,
        mesh=mesh,
        in_specs=(
            P(None, REP_GX),
            P(REP_GX),
            P(None, REP_GX),
            P(REP_GX),
            P(REP_GX, None),
            P(None, REP_GX, None),
        ),
        out_specs=(P(None, REP_GX), P(None, REP_GX)),
        check_vma=False,
    )
```

time: 178 us -> 150 us (0.84); the launches traced: 176 us -> 150 us
  waiting for transfers between devices: 22.6 us -> 8.18 us
  starting transfers between devices: 50.9 us -> 41.9 us
  local copies, waits for them, and re-layouts: 5.53 us -> 2.04 us
    ppermute x4, starting transfers between devices: 37.4 us -> 28.9 us  [swap(): lax.ppermute(value, 'gx', near_pairs)]
    ppermute x4, waiting for transfers between devices: 7.93 us -> 0.01 us  [swap(): lax.ppermute(value, 'gx', far_pairs)]
    unnamed x12 -> x6, local copies, waits for them, and re-layouts: 4.65 us -> 1.37 us
    all_to_all x1, waiting for transfers between devices: 11.4 us -> 8.16 us  [on_device(): lax.all_to_all(jnp.broadcast_to(gram, (slabs, width)), 'gx', 0, 0, tiled=...]
    ppermute x4, waiting for transfers between devices: 2.64 us -> 0.01 us  [swap(): lax.ppermute(value, 'gx', near_pairs)]
    all_to_all x1, starting transfers between devices: 11.7 us -> 9.07 us  [on_device(): lax.all_to_all(jnp.broadcast_to(gram, (slabs, width)), 'gx', 0, 0, tiled=...]
    ppermute x4, starting transfers between devices: 0.01 us -> 2.16 us  [swap(): lax.ppermute(value, 'gx', far_pairs)]
    pallas_call x6 -> x12, Pallas kernels: 91.6 us -> 93.1 us  [the longest x4 38.7 us: apply(): pl.pallas_call(functools.partial(cross_apply_kernel, start=start, inv_sta...]
  transfers between devices with their start and end apart: 10 -> 11, of which waited for: 8 -> 1; matrix products, arithmetic and copies ran while one was open for 1% -> 0% of each run, Pallas kernels for 0% -> 23%
where the time goes in v2:
time: 150 us
  Pallas kernels  96.5 us (64%)
  starting transfers between devices  41.9 us (28%)
  waiting for transfers between devices  8.18 us (5%)
  local copies, waits for them, and re-layouts  2.04 us (1%)
    pallas_call x4, Pallas kernels, apply(): pl.pallas_call(functools.partial(cross_apply_kernel, start=start, inv_sta...  38.7 us
    ppermute x4, starting transfers between devices, swap(): lax.ppermute(value, 'gx', near_pairs)  28.9 us
    pallas_call x4, Pallas kernels, apply(): pl.pallas_call(functools.partial(local_apply_kernel, start=start), out_sh...  27.7 us
    pallas_call x1, Pallas kernels, on_device(): pl.pallas_call(functools.partial(cross_pairs_kernel, boxes=boxes), out_sh...  13 us
    pallas_call x1, Pallas kernels, on_device(): pl.pallas_call(functools.partial(local_pairs_kernel, boxes=boxes), out_sh...  9.46 us
    all_to_all x1, starting transfers between devices, on_device(): lax.all_to_all(jnp.broadcast_to(gram, (slabs, width)), 'gx', 0, 0, tiled=...  9.07 us
    all_to_all x1, waiting for transfers between devices, on_device(): lax.all_to_all(jnp.broadcast_to(gram, (slabs, width)), 'gx', 0, 0, tiled=...  8.16 us
    pallas_call x1, Pallas kernels, on_device(): pl.pallas_call(functools.partial(untile_kernel, start=start), out_shape=(...  3.24 us
  transfers between devices with their start and end apart: 11, of which 1 were waited for; matrix products, arithmetic and copies ran while one was open for 0% of the time, Pallas kernels for 23%

profile of v2, /device:TPU:513, one launch (start us, length us, event | category | flops | bytes accessed | tf_op | source)
XLA Modules:
  0.0 149.5 jit_solution(6933568798494287633)
XLA Ops:
  0.6 2.5 %tile_in.1.own_ref.inv_ref.refs_0_ = f32[256,128]{1,0:T(8,128)S(1)} custom-call(f32[3,4096]{1,0:T(4,128)} %pos_hbm.1, f32[1,4096]{1,0:T(1,128)} %bitcast.17, f32[3,4096]{1,0:T(4,128)} %fld_hbm.1, s32[32,128]{1,0:T(8,128)} %bitcast.10), custom_call_target="tpu_custom_call" | custom-call | tf_op jit(solution)/shard_map/tile_in/pallas_call | solution.py:579
  3.1 20.5 %collective-permute-start.2 = (f32[256,128]{1,0:T(8,128)S(1)}, f32[256,128]{1,0:T(8,128)S(1)}, u32[]{:S(2)}, u32[]{:S(2)}) collective-permute-start(f32[256,128]{1,0:T(8,128)S(1)} %tile_in.1.own_ref.inv_ref.refs_0_), channel_id=1, source_target_pairs={{0,1},{1,0},{2,3},{3,2},{4,5},{5,4},{6,7},{7,6},{8,9},{9,8},{10,11... | collective-permute-start | bytes 393224 | tf_op jit(solution)/shard_map/ppermute | solution.py:570
  23.6 0.0 collective-permute-start.3
  23.6 1.7 %collective-permute-start.1 = (s32[3,2,32]{2,1,0:T(2,128)}, s32[3,2,32]{2,1,0:T(2,128)S(1)}, u32[]{:S(2)}, u32[]{:S(2)}) collective-permute-start(s32[3,2,32]{2,1,0:T(2,128)} %bitcast.13), channel_id=1, source_target_pairs={{0,1},{1,2},{2,3},{3,4},{4,5},{5,6},{6,7},{7,8},{8,9},{9,10},{10,1... | collective-permute-start | bytes 2312 | tf_op jit(solution)/shard_map/ppermute | solution.py:575
  25.4 0.0 collective-permute-start
  25.4 0.1 pad_add_fusion.par_ref
  25.5 0.0 copy-start.1
  25.5 0.7 copy-done.1
  26.2 0.0 copy-start.2
  26.2 0.7 copy-done.2
  26.9 9.5 %local_pairs.1 = (f32[49664,128]{1,0:T(8,128)S(1)}, s32[3,65]{1,0:T(4,128)S(1)}) custom-call(s32[3,32]{1,0:T(4,128)S(1)} %bitcast.16, s32[3,2,32]{2,1,0:T(2,128)S(1)} %bitcast.14, f32[256,128]{1,0:T(8,128)S(1)} %tile_in.1.own_ref.inv_ref.refs_0_), custom_call_target="tpu_custom_call" | custom-call | flops 60000000 | bytes 1000000 | tf_op jit(solution)/shard_map/local_pairs/pallas_call | solution.py:607
  36.3 0.0 collective-permute-done.prev_list
  36.3 0.0 collective-permute-done.1.prev_shift
  36.3 0.0 collective-permute-done.2.near_ref
  36.4 0.0 collective-permute-done.3.far_ref
  36.4 13.0 %cross_pairs.1 = (f32[49664,128]{1,0:T(8,128)S(1)}, f32[33280,128]{1,0:T(8,128)}, s32[3,65]{1,0:T(4,128)S(1)}) custom-call(s32[3]{0:T(128)S(1)} %pad_add_fusion.par_ref, s32[3,65]{1,0:T(4,128)S(1)} %get-tuple-element.12.own_tab.tab_ref, s32[3,32]{1,0:T(4,128)S(1)} %collective-permute-done.prev_list, ...), custom_call_target="tpu_custom_call", output_to_operand_aliasing={{0}: (7, {})} | custom-call | flops 60000000 | bytes 1000000 | tf_op jit(solution)/shard_map/cross_pairs/pallas_call | solution.py:617
  49.4 6.9 %local_apply.4.part_ref = f32[96,128]{1,0:T(8,128)S(1)} custom-call(s32[3,65]{1,0:T(4,128)S(1)} %get-tuple-element.12.own_tab.tab_ref, f32[49664,128]{1,0:T(8,128)S(1)} %get-tuple-element.15.tensor_ref, f32[256,128]{1,0:T(8,128)S(1)} %tile_in.1.own_ref.inv_ref.refs_0_), custom_call_target="tpu_custom_call" | custom-call | flops 60000000 | bytes 1000000 | tf_op jit(solution)/shard_map/local_apply/pallas_call | solution.py:641
  56.3 9.7 %cross_apply.4.own_ref.refs_1_ = f32[96,128]{1,0:T(8,128)S(1)} custom-call(s32[3]{0:T(128)S(1)} %pad_add_fusion.par_ref, s32[3,65]{1,0:T(4,128)S(1)} %get-tuple-element.12.own_tab.tab_ref, s32[3,65]{1,0:T(4,128)S(1)} %get-tuple-element.14.prev_tab, f32[49664,128]{1,0:T(8,128)S(1)} %get-tuple-element.15.tensor_ref, f32[33280,128]{1,0:T(8,128)} %get-tuple-element.16.prev_hbm, ...), custom_call_target="tpu_custom_call" | custom-call | flops 60000000 | bytes 1000000 | tf_op jit(solution)/shard_map/cross_apply/pallas_call | solution.py:651
  66.0 1.6 %collective-permute-start.4 = (f32[96,128]{1,0:T(8,128)S(1)}, f32[96,128]{1,0:T(8,128)S(1)}, u32[]{:S(2)}, u32[]{:S(2)}) collective-permute-start(f32[96,128]{1,0:T(8,128)S(1)} %cross_apply.4.own_ref.refs_1_), channel_id=1, source_target_pairs={{0,1},{1,0},{2,3},{3,2},{4,5},{5,4},{6,7},{7,6},{8,9},{9,8},{10,11... | collective-permute-start | bytes 147464 | tf_op jit(solution)/shard_map/ppermute | solution.py:570
  67.6 0.7 collective-permute-start.5
  68.3 6.9 %local_apply.5.part_ref = f32[96,128]{1,0:T(8,128)S(1)} custom-call(s32[3,65]{1,0:T(4,128)S(1)} %get-tuple-element.12.own_tab.tab_ref, f32[49664,128]{1,0:T(8,128)S(1)} %get-tuple-element.15.tensor_ref, f32[96,128]{1,0:T(8,128)S(1)} %cross_apply.4.own_ref.refs_1_), custom_call_target="tpu_custom_call" | custom-call | flops 60000000 | bytes 1000000 | tf_op jit(solution)/shard_map/local_apply/pallas_call | solution.py:641
  75.2 0.0 collective-permute-done.4.near_ref
  75.2 0.0 collective-permute-done.5.far_ref
  75.2 9.7 %cross_apply.5.own_ref.refs_2_ = f32[96,128]{1,0:T(8,128)S(1)} custom-call(s32[3]{0:T(128)S(1)} %pad_add_fusion.par_ref, s32[3,65]{1,0:T(4,128)S(1)} %get-tuple-element.12.own_tab.tab_ref, s32[3,65]{1,0:T(4,128)S(1)} %get-tuple-element.14.prev_tab, f32[49664,128]{1,0:T(8,128)S(1)} %get-tuple-element.15.tensor_ref, f32[33280,128]{1,0:T(8,128)} %get-tuple-element.16.prev_hbm, ...), custom_call_target="tpu_custom_call" | custom-call | flops 60000000 | bytes 1000000 | tf_op jit(solution)/shard_map/cross_apply/pallas_call | solution.py:651
  84.9 4.8 %collective-permute-start.6 = (f32[96,128]{1,0:T(8,128)S(1)}, f32[96,128]{1,0:T(8,128)S(1)}, u32[]{:S(2)}, u32[]{:S(2)}) collective-permute-start(f32[96,128]{1,0:T(8,128)S(1)} %cross_apply.5.own_ref.refs_2_), channel_id=1, source_target_pairs={{0,1},{1,0},{2,3},{3,2},{4,5},{5,4},{6,7},{7,6},{8,9},{9,8},{10,11... | collective-permute-start | bytes 147464 | tf_op jit(solution)/shard_map/ppermute | solution.py:570
  89.6 0.0 collective-permute-start.7
  89.6 6.9 %local_apply.6.part_ref = f32[96,128]{1,0:T(8,128)S(1)} custom-call(s32[3,65]{1,0:T(4,128)S(1)} %get-tuple-element.12.own_tab.tab_ref, f32[49664,128]{1,0:T(8,128)S(1)} %get-tuple-element.15.tensor_ref, f32[96,128]{1,0:T(8,128)S(1)} %cross_apply.5.own_ref.refs_2_), custom_call_target="tpu_custom_call" | custom-call | flops 60000000 | bytes 1000000 | tf_op jit(solution)/shard_map/local_apply/pallas_call | solution.py:641
  96.5 0.0 collective-permute-done.6.near_ref
  96.5 0.0 collective-permute-done.7.far_ref
  96.5 9.7 %cross_apply.6.own_ref.refs_3_ = f32[96,128]{1,0:T(8,128)S(1)} custom-call(s32[3]{0:T(128)S(1)} %pad_add_fusion.par_ref, s32[3,65]{1,0:T(4,128)S(1)} %get-tuple-element.12.own_tab.tab_ref, s32[3,65]{1,0:T(4,128)S(1)} %get-tuple-element.14.prev_tab, f32[49664,128]{1,0:T(8,128)S(1)} %get-tuple-element.15.tensor_ref, f32[33280,128]{1,0:T(8,128)} %get-tuple-element.16.prev_hbm, ...), custom_call_target="tpu_custom_call" | custom-call | flops 60000000 | bytes 1000000 | tf_op jit(solution)/shard_map/cross_apply/pallas_call | solution.py:651
  106.2 2.0 %collective-permute-start.8 = (f32[96,128]{1,0:T(8,128)S(1)}, f32[96,128]{1,0:T(8,128)S(1)}, u32[]{:S(2)}, u32[]{:S(2)}) collective-permute-start(f32[96,128]{1,0:T(8,128)S(1)} %cross_apply.6.own_ref.refs_3_), channel_id=1, source_target_pairs={{0,1},{1,0},{2,3},{3,2},{4,5},{5,4},{6,7},{7,6},{8,9},{9,8},{10,11... | collective-permute-start | bytes 147464 | tf_op jit(solution)/shard_map/ppermute | solution.py:570
  108.2 1.5 %collective-permute-start.9 = (f32[96,128]{1,0:T(8,128)S(1)}, f32[96,128]{1,0:T(8,128)S(1)}, u32[]{:S(2)}, u32[]{:S(2)}) collective-permute-start(f32[96,128]{1,0:T(8,128)S(1)} %cross_apply.6.own_ref.refs_3_), channel_id=1, source_target_pairs={{0,127},{1,2},{2,1},{3,4},{4,3},{5,6},{6,5},{7,8},{8,7},{9,10},{10... | collective-permute-start | bytes 147464 | tf_op jit(solution)/shard_map/ppermute | solution.py:570
  109.7 7.1 %local_apply.7.part_ref = f32[96,128]{1,0:T(8,128)S(1)} custom-call(s32[3,65]{1,0:T(4,128)S(1)} %get-tuple-element.12.own_tab.tab_ref, f32[49664,128]{1,0:T(8,128)S(1)} %get-tuple-element.15.tensor_ref, f32[96,128]{1,0:T(8,128)S(1)} %cross_apply.6.own_ref.refs_3_), custom_call_target="tpu_custom_call" | custom-call | flops 60000000 | bytes 1000000 | tf_op jit(solution)/shard_map/local_apply/pallas_call | solution.py:641
  116.8 0.0 copy-start
  116.8 0.0 collective-permute-done.8.near_ref
  116.8 0.0 collective-permute-done.9.far_ref
  116.8 9.7 %cross_apply.7.refs_4_ = f32[96,128]{1,0:T(8,128)S(1)} custom-call(s32[3]{0:T(128)S(1)} %pad_add_fusion.par_ref, s32[3,65]{1,0:T(4,128)S(1)} %get-tuple-element.12.own_tab.tab_ref, s32[3,65]{1,0:T(4,128)S(1)} %get-tuple-element.14.prev_tab, f32[49664,128]{1,0:T(8,128)S(1)} %get-tuple-element.15.tensor_ref, f32[33280,128]{1,0:T(8,128)} %get-tuple-element.16.prev_hbm, ...), custom_call_target="tpu_custom_call" | custom-call | flops 60000000 | bytes 1000000 | tf_op jit(solution)/shard_map/cross_apply/pallas_call | solution.py:651
  126.5 0.1 gram.1
  126.6 0.7 broadcast_in_dim.2
  127.3 9.1 %all-to-all-start = ((f32[128,1,128]{2,1,0:T(1,128)}), f32[128,1,128]{2,1,0:T(1,128)S(1)}, u32[]{:S(2)}, u32[]{:S(2)}) async-start(f32[128,1,128]{2,1,0:T(1,128)} %broadcast_in_dim.2), calls=%async_computation | async-start | bytes 131072 | tf_op jit(solution)/shard_map/all_to_all | solution.py:683
  136.4 0.0 copy-done
  136.4 0.8 inverse.1.inv_ref
  137.2 3.2 %untile.1 = (f32[3,4096]{1,0:T(4,128)S(1)}, f32[3,4096]{1,0:T(4,128)S(1)}, f32[3,4096]{1,0:T(4,128)S(1)}, f32[3,4096]{1,0:T(4,128)S(1)}, f32[3,4096]{1,0:T(4,128)S(1)}) custom-call(s32[32,128]{1,0:T(8,128)S(1)} %inverse.1.inv_ref, f32[256,128]{1,0:T(8,128)S(1)} %tile_in.1.own_ref.inv_ref.refs_0_, f32[96,128]{1,0:T(8,128)S(1)} %cross_apply.4.own_ref.refs_1_, ...), custom_call_target="tpu_custom_call" | custom-call | flops 60000000 | bytes 1000000 | tf_op jit(solution)/shard_map/untile/pallas_call | solution.py:684
  140.5 8.2 %all-to-all-done = f32[128,1,128]{2,1,0:T(1,128)S(1)} async-done(((f32[128,1,128]{2,1,0:T(1,128)}), f32[128,1,128]{2,1,0:T(1,128)S(1)}, u32[]{:S(2)}, u32[]{:S(2)}) %all-to-all-start) | async-done | bytes 65568 | tf_op jit(solution)/shard_map/all_to_all | solution.py:683
  148.6 0.9 outputs.1
Async XLA Ops:
  3.1 33.2 %collective-permute-start.2 = (f32[256,128]{1,0:T(8,128)S(1)}, f32[256,128]{1,0:T(8,128)S(1)}, u32[]{:S(2)}, u32[]{:S(2)}) collective-permute-start(f32[256,128]{1,0:T(8,128)S(1)} %tile_in.1.own_ref.inv_ref.refs_0_), channel_id=1, source_target_pairs={{0,1},{1,0},{2,3},{3,2},{4,5},{5,4},{6,7},{7,6},{8,9},{9,8},{10,11... | collective-permute-start | bytes 393224 | tf_op jit(solution)/shard_map/ppermute | solution.py:570
  23.6 12.7 %collective-permute-start.3 = (f32[256,128]{1,0:T(8,128)S(1)}, f32[256,128]{1,0:T(8,128)S(1)}, u32[]{:S(2)}, u32[]{:S(2)}) collective-permute-start(f32[256,128]{1,0:T(8,128)S(1)} %tile_in.1.own_ref.inv_ref.refs_0_), channel_id=1, source_target_pairs={{0,127},{1,2},{2,1},{3,4},{4,3},{5,6},{6,5},{7,8},{8,7},{9,10},{10... | collective-permute-start | bytes 393224 | tf_op jit(solution)/shard_map/ppermute | solution.py:570
  23.6 12.7 %collective-permute-start.1 = (s32[3,2,32]{2,1,0:T(2,128)}, s32[3,2,32]{2,1,0:T(2,128)S(1)}, u32[]{:S(2)}, u32[]{:S(2)}) collective-permute-start(s32[3,2,32]{2,1,0:T(2,128)} %bitcast.13), channel_id=1, source_target_pairs={{0,1},{1,2},{2,3},{3,4},{4,5},{5,6},{6,7},{7,8},{8,9},{9,10},{10,1... | collective-permute-start | bytes 2312 | tf_op jit(solution)/shard_map/ppermute | solution.py:575
  25.4 10.9 %collective-permute-start = (s32[3,32]{1,0:T(4,128)}, s32[3,32]{1,0:T(4,128)S(1)}, u32[]{:S(2)}, u32[]{:S(2)}) collective-permute-start(s32[3,32]{1,0:T(4,128)} %bitcast.15), channel_id=1, source_target_pairs={{0,1},{1,2},{2,3},{3,4},{4,5},{5,6},{6,7},{7,8},{8,9},{9,10},{10,1... | collective-permute-start | bytes 1160 | tf_op jit(solution)/shard_map/ppermute | solution.py:574
  25.5 0.7 copy-start.1
  26.2 0.7 copy-start.2
  66.0 9.2 %collective-permute-start.4 = (f32[96,128]{1,0:T(8,128)S(1)}, f32[96,128]{1,0:T(8,128)S(1)}, u32[]{:S(2)}, u32[]{:S(2)}) collective-permute-start(f32[96,128]{1,0:T(8,128)S(1)} %cross_apply.4.own_ref.refs_1_), channel_id=1, source_target_pairs={{0,1},{1,0},{2,3},{3,2},{4,5},{5,4},{6,7},{7,6},{8,9},{9,8},{10,11... | collective-permute-start | bytes 147464 | tf_op jit(solution)/shard_map/ppermute | solution.py:570
  67.6 7.6 %collective-permute-start.5 = (f32[96,128]{1,0:T(8,128)S(1)}, f32[96,128]{1,0:T(8,128)S(1)}, u32[]{:S(2)}, u32[]{:S(2)}) collective-permute-start(f32[96,128]{1,0:T(8,128)S(1)} %cross_apply.4.own_ref.refs_1_), channel_id=1, source_target_pairs={{0,127},{1,2},{2,1},{3,4},{4,3},{5,6},{6,5},{7,8},{8,7},{9,10},{10... | collective-permute-start | bytes 147464 | tf_op jit(solution)/shard_map/ppermute | solution.py:570
  84.9 11.6 %collective-permute-start.6 = (f32[96,128]{1,0:T(8,128)S(1)}, f32[96,128]{1,0:T(8,128)S(1)}, u32[]{:S(2)}, u32[]{:S(2)}) collective-permute-start(f32[96,128]{1,0:T(8,128)S(1)} %cross_apply.5.own_ref.refs_2_), channel_id=1, source_target_pairs={{0,1},{1,0},{2,3},{3,2},{4,5},{5,4},{6,7},{7,6},{8,9},{9,8},{10,11... | collective-permute-start | bytes 147464 | tf_op jit(solution)/shard_map/ppermute | solution.py:570
  89.6 6.9 %collective-permute-start.7 = (f32[96,128]{1,0:T(8,128)S(1)}, f32[96,128]{1,0:T(8,128)S(1)}, u32[]{:S(2)}, u32[]{:S(2)}) collective-permute-start(f32[96,128]{1,0:T(8,128)S(1)} %cross_apply.5.own_ref.refs_2_), channel_id=1, source_target_pairs={{0,127},{1,2},{2,1},{3,4},{4,3},{5,6},{6,5},{7,8},{8,7},{9,10},{10... | collective-permute-start | bytes 147464 | tf_op jit(solution)/shard_map/ppermute | solution.py:570
  106.2 10.5 %collective-permute-start.8 = (f32[96,128]{1,0:T(8,128)S(1)}, f32[96,128]{1,0:T(8,128)S(1)}, u32[]{:S(2)}, u32[]{:S(2)}) collective-permute-start(f32[96,128]{1,0:T(8,128)S(1)} %cross_apply.6.own_ref.refs_3_), channel_id=1, source_target_pairs={{0,1},{1,0},{2,3},{3,2},{4,5},{5,4},{6,7},{7,6},{8,9},{9,8},{10,11... | collective-permute-start | bytes 147464 | tf_op jit(solution)/shard_map/ppermute | solution.py:570
  108.2 8.6 %collective-permute-start.9 = (f32[96,128]{1,0:T(8,128)S(1)}, f32[96,128]{1,0:T(8,128)S(1)}, u32[]{:S(2)}, u32[]{:S(2)}) collective-permute-start(f32[96,128]{1,0:T(8,128)S(1)} %cross_apply.6.own_ref.refs_3_), channel_id=1, source_target_pairs={{0,127},{1,2},{2,1},{3,4},{4,3},{5,6},{6,5},{7,8},{8,7},{9,10},{10... | collective-permute-start | bytes 147464 | tf_op jit(solution)/shard_map/ppermute | solution.py:570
  116.8 19.6 %copy-start = (s32[4096]{0:T(1024)S(1)}, s32[4096]{0:T(1024)}, u32[]{:S(2)}) copy-start(s32[4096]{0:T(1024)} %param.9) | copy-start | bytes 49156
  127.3 21.3 %all-to-all-start = ((f32[128,1,128]{2,1,0:T(1,128)}), f32[128,1,128]{2,1,0:T(1,128)S(1)}, u32[]{:S(2)}, u32[]{:S(2)}) async-start(f32[128,1,128]{2,1,0:T(1,128)} %broadcast_in_dim.2), calls=%async_computation | async-start | bytes 131072 | tf_op jit(solution)/shard_map/all_to_all | solution.py:683

commit v3 on v2

v3 whole, which is shorter than its diff:
```python
import functools

import jax
import jax.numpy as jnp
from jax import lax
from jax.experimental import pallas as pl
from jax.experimental.pallas import tpu as pltpu
from jax.sharding import PartitionSpec as P

ITERS = 4
REP_GX = ("rep", "gx")
THOLE = 0.39
SHIFT = 2.5
SCALE = 1.5
MATS = 4
OUT_SLOTS = 12
BATCH = 8
HALF = 4
PAD = 12
GROUP = 16
SLOTS = 24
MIB = 2**20

F32 = jnp.float32
VMEM = pl.BlockSpec(memory_space=pltpu.VMEM)
SMEM = pl.BlockSpec(memory_space=pltpu.SMEM)
HBM = pl.BlockSpec(memory_space=pltpu.MemorySpace.HBM)


def spread(row, height=8):
    return jnp.broadcast_to(row, (height, row.shape[1]))


def lane_pick(row_block, lanes):
    return jnp.take_along_axis(row_block, lanes, axis=1)


def params(mib):
    return pltpu.CompilerParams(vmem_limit_bytes=mib * MIB)


def tile_in_kernel(pos_hbm, pol_hbm, fld_hbm, idx_hbm, out_ref, pos_ref, pol_ref, fld_ref, idx_ref, sems):
    copies = [
        pltpu.make_async_copy(source, target, sems.at[k])
        for k, (source, target) in enumerate(
            ((idx_hbm, idx_ref), (pos_hbm, pos_ref), (pol_hbm, pol_ref), (fld_hbm, fld_ref))
        )
    ]
    for copy in copies:
        copy.start()
    for copy in copies:
        copy.wait()
    tiles, width = idx_ref.shape
    for q in range(tiles // 8):
        rows = idx_ref[8 * q : 8 * q + 8, :]
        high = rows // width
        low = rows - high * width

        def step(h, acc):
            at = pl.ds(pl.multiple_of(h * width, width), width)
            hit = high == h
            new = []
            for c in range(7):
                if c < 3:
                    row = pos_ref[c : c + 1, at]
                elif c == 3:
                    row = pol_ref[0:1, at]
                else:
                    row = fld_ref[c - 4 : c - 3, at]
                new.append(jnp.where(hit, lane_pick(spread(row), low), acc[c]))
            return tuple(new)

        acc = lax.fori_loop(0, tiles, step, (jnp.zeros((8, width), F32),) * 7, unroll=16)
        values = list(acc[:3]) + [lax.rsqrt(acc[3])] + list(acc[4:]) + [1.0 / acc[3]]
        for c in range(8):
            out_ref[c * tiles + 8 * q : c * tiles + 8 * q + 8, :] = values[c]


def inverse_kernel(idx_ref, out_ref):
    tiles, width = idx_ref.shape
    total = jnp.zeros((2 * tiles, width), F32)
    lane = lax.broadcasted_iota(jnp.int32, (tiles, width), 1).astype(F32)
    row_id = lax.broadcasted_iota(jnp.int32, (tiles, width), 0)
    low_id = lax.broadcasted_iota(jnp.int32, (width, width), 0)
    for t in range(tiles):
        row = idx_ref[t : t + 1, :]
        high = row // width
        low = row - high * width
        hit = spread(high, tiles) == row_id
        left = jnp.concatenate([jnp.where(hit, float(t), 0.0), jnp.where(hit, lane, 0.0)], axis=0)
        right = jnp.where(spread(low, width) == low_id, 1.0, 0.0)
        total = total + lax.dot_general(
            left.astype(jnp.bfloat16),
            right.astype(jnp.bfloat16),
            (((1,), (1,)), ((), ())),
            preferred_element_type=F32,
        )
    out_ref[...] = (total[:tiles] * float(width) + total[tiles:] + 0.5).astype(jnp.int32)


def pair_coefficients(off, ri, rj, same):
    dist_sq = off[0] * off[0] + off[1] * off[1] + off[2] * off[2]
    if same is not None:
        dist_sq = jnp.where(same, 1.0, dist_sq)
    inv = lax.rsqrt(dist_sq)
    damp = (dist_sq * (dist_sq * inv)) * (THOLE * ri * rj)
    decay = jnp.exp(-damp)
    inv_sq = inv * inv
    cube = inv_sq * inv
    g3 = (1.0 - decay) * cube
    g5 = (3.0 - (3.0 + 3.0 * damp) * decay) * (cube * inv_sq)
    root = g5 * lax.rsqrt(g5)
    if same is not None:
        g3 = jnp.where(same, 0.0, g3)
        root = jnp.where(same, 0.0, root)
    return [root * off[0], root * off[1], root * off[2], g3]


def split_rows(a_ref, first_tile, ref, first, tiles, comps):
    for c in range(comps):
        rest = ref[first + c * tiles : first + (c + 1) * tiles, :]
        for k in range(3):
            part = rest.astype(jnp.bfloat16).astype(F32) if k < 2 else rest
            a_ref[pl.ds(first_tile * GROUP + 3 * c + k, tiles, stride=GROUP), :] = part
            rest = rest - part


def selector(comps, width):
    k = lax.broadcasted_iota(jnp.int32, (GROUP, comps * width), 0)
    lane = lax.broadcasted_iota(jnp.int32, (GROUP, comps * width), 1)
    first = lane // width * 3
    return jnp.where(jnp.logical_and(k >= first, k < first + 3), 1.0, 0.0).astype(jnp.bfloat16)


def turn_rows(at_ref, a_ref):
    width = a_ref.shape[1]

    def turn(t, _):
        part = a_ref[pl.ds(pl.multiple_of(t * GROUP, GROUP), GROUP), :].astype(jnp.bfloat16)
        at_ref[pl.ds(pl.multiple_of(t * width, width), width), :] = part.T
        return 0

    lax.fori_loop(0, a_ref.shape[0] // GROUP, turn, 0, unroll=8)


def write_columns(col_ref, place, at_ref, tile, select):
    width = col_ref.shape[0] // HALF
    part = at_ref[pl.ds(pl.multiple_of(tile * width, width), width), :]
    col_ref[place * width : (place + 1) * width, :] = jnp.dot(part, select, preferred_element_type=F32)


def pipelined(count, columns, compute, cols, before=None, after=None):
    first, second = cols
    columns(0, first)

    def body(i, _):
        if before is not None:
            before(i)
        columns(2 * i + 1, second)
        compute(2 * i, first, 0)
        columns(2 * i + 2, first)
        compute(2 * i + 1, second, 1)
        if after is not None:
            after(i)
        return 0

    lax.fori_loop(0, (count + BATCH - 1) // BATCH, body, 0)


def pack_job(t, n, slot, y, z, spare=0):
    return t + n * 256 + slot * 65536 + (y + 2 * z + 4 * spare) * 16777216


def pad_jobs(tab_ref, line, count, slot, y, z):
    for k in range(PAD):
        tab_ref[line, count + k] = pack_job(0, 0, slot, y, z, 1)


def target_source(word):
    return word & 255, (word >> 8) & 255


def row_block(ref, tiles, n, count):
    return [spread(ref[pl.ds(c * tiles + n, 1), :]) for c in range(count)]


def pair_block(col_ref, place, row, kind, lead, store):
    width = row[0].shape[1]
    if kind == "row":
        row = [row[c] + lead[c] for c in range(3)] + [row[3]]
    for k in range(width // 8):
        first = place * width + 8 * k
        col = [col_ref[first : first + 8, c * width : (c + 1) * width] for c in range(4)]
        if kind == "col":
            off = [(col[c] + lead[c]) - row[c] for c in range(3)]
        else:
            off = [row[c] - col[c] for c in range(3)]
        mask = None
        if kind == "self":
            i = lax.broadcasted_iota(jnp.int32, (8, width), 0) + 8 * k
            j = lax.broadcasted_iota(jnp.int32, (8, width), 1)
            mask = i == j
        store(k, pair_coefficients(off, col[3], row[3], mask))


def store_at(ref, base):
    width = ref.shape[1]

    def store(k, mats):
        for m in range(MATS):
            ref[pl.ds(base + m * width + 8 * k, 8), :] = mats[m]

    return store


def rounded(count):
    return (count + BATCH - 1) // BATCH * BATCH


class Stream:
    def __init__(self, hbm, slots, sems, size, depth, inward):
        self.parts = (hbm, slots, sems, size, depth, inward)

    def base(self, i):
        _, _, _, size, depth, _ = self.parts
        return pl.multiple_of(lax.rem(i, depth) * size, size)

    def copy(self, i):
        hbm, slots, sems, size, depth, inward = self.parts
        far = hbm.at[pl.ds(pl.multiple_of(i * size, size), size), :]
        near = slots.at[pl.ds(self.base(i), size), :]
        sem = sems.at[lax.rem(i, depth)]
        return pltpu.make_async_copy(far, near, sem) if inward else pltpu.make_async_copy(near, far, sem)

    def start(self, low, high):
        def one(i, _):
            self.copy(i).start()
            return 0

        lax.fori_loop(low, high, one, 0)

    def wait(self, low, high):
        def one(i, _):
            self.copy(i).wait()
            return 0

        lax.fori_loop(low, high, one, 0)


def make_pairs(tab_ref, line, count, at_ref, a_first, own_ref, cols, select, kind, boxes, wrap, target, stream=None):
    tiles = own_ref.shape[0] // 8
    width = own_ref.shape[1]
    size = MATS * width

    def columns(j, col_ref):
        for p in range(HALF):
            _, n = target_source(tab_ref[line, HALF * j + p])
            write_columns(col_ref, p, at_ref, a_first + n, select)

    def compute(j, col_ref, _half):
        for p in range(HALF):
            word = tab_ref[line, HALF * j + p]
            t, _ = target_source(word)
            last = word >> 24
            lead = (wrap, (last & 1).astype(F32) * boxes[1], ((last >> 1) & 1).astype(F32) * boxes[2])
            if stream is None:
                base = pl.multiple_of(((word >> 16) & 255) * size, size)
            else:
                base = stream.base(HALF * j + p)
            pair_block(col_ref, p, row_block(own_ref, tiles, t, 4), kind, lead, store_at(target, base))

    if stream is None:
        pipelined(count, columns, compute, cols)
        return
    depth = stream.parts[4]

    def before(i):
        for p in range(BATCH):

            @pl.when(BATCH * i + p >= depth)
            def _():
                stream.copy(BATCH * i + p - depth).wait()

    def after(i):
        for p in range(BATCH):
            stream.copy(BATCH * i + p).start()

    pipelined(count, columns, compute, cols, before, after)


def local_pairs_kernel(
    own_list, own_shift, own_ref, tensor_ref, back_hbm, tab_ref, a_ref, at_ref, col_a, col_b, slots, sems, *, boxes
):
    tiles = own_ref.shape[0] // 8
    width = own_ref.shape[1]
    extra = own_list.shape[0] - 1
    cap = extra * tiles
    size = MATS * width
    for t in range(tiles):
        tab_ref[1, t] = pack_job(t, t, t, 0, 0)

    def sort(k, counts):
        inner, outer = counts
        e = k // tiles
        t = k - e * tiles
        n = own_list[1 + e, t]
        y = own_shift[1 + e, 0, t]
        z = own_shift[1 + e, 1, t]
        near = (n < tiles).astype(jnp.int32)
        tab_ref[1, tiles + inner] = pack_job(n * near, t, tiles + k, y, z)
        tab_ref[2, outer] = pack_job(t, n - tiles * (1 - near), tiles + k, y, z)
        tab_ref[3, inner] = pack_job(t, n * near, 0, y, z)
        return inner + near, outer + 1 - near

    inner, outer = lax.fori_loop(0, cap, sort, (jnp.int32(0), jnp.int32(0)), unroll=8)
    pad_jobs(tab_ref, 1, tiles + inner, tiles + cap, 1, 1)
    pad_jobs(tab_ref, 2, outer, tiles + cap, 1, 1)
    pad_jobs(tab_ref, 3, inner, 0, 1, 1)
    tab_ref[0, 0] = inner
    tab_ref[0, 1] = outer
    a_ref[...] = jnp.zeros_like(a_ref)
    split_rows(a_ref, 0, own_ref, 0, tiles, 4)
    turn_rows(at_ref, a_ref)
    select = selector(4, width)
    cols = (col_a, col_b)
    make_pairs(tab_ref, 1, tiles, at_ref, 0, own_ref, cols, select, "self", boxes, 0.0, tensor_ref)
    stream = Stream(back_hbm, slots, sems, size, OUT_SLOTS, False)
    make_pairs(tab_ref, 3, inner, at_ref, 0, own_ref, cols, select, "col", boxes, 0.0, slots, stream)

    def shifted_columns(j, col_ref):
        for p in range(HALF):
            _, n = target_source(tab_ref[1, tiles + HALF * j + p])
            write_columns(col_ref, p, at_ref, n, select)

    def shifted_compute(j, col_ref, _half):
        for p in range(HALF):
            word = tab_ref[1, tiles + HALF * j + p]
            t, _ = target_source(word)
            last = word >> 24
            lead = (0.0, (last & 1).astype(F32) * boxes[1], ((last >> 1) & 1).astype(F32) * boxes[2])
            base = pl.multiple_of(((word >> 16) & 255) * size, size)
            pair_block(col_ref, p, row_block(own_ref, tiles, t, 4), "row", lead, store_at(tensor_ref, base))

    pipelined(inner, shifted_columns, shifted_compute, cols)
    done = rounded(inner)
    stream.wait(jnp.maximum(done - OUT_SLOTS, 0), done)


def cross_pairs_kernel(
    par_ref, own_tab, prev_list, prev_shift, own_ref, near_ref, far_ref, tensor_in,
    tensor_ref, prev_hbm, tab_ref, a_ref, at_ref, col_a, col_b, slots, sems,
    *, boxes,
):
    del tensor_in
    tiles = own_ref.shape[0] // 8
    width = own_ref.shape[1]
    extra = prev_list.shape[0] - 1
    cap = extra * tiles
    size = MATS * width
    par = par_ref[0]
    wrap_next = par_ref[1].astype(F32) * boxes[0]
    wrap_prev = par_ref[2].astype(F32) * boxes[0]
    a_ref[...] = jnp.zeros_like(a_ref)
    split_rows(a_ref, par * tiles, near_ref, 0, tiles, 4)
    split_rows(a_ref, (1 - par) * tiles, far_ref, 0, tiles, 4)

    def sort(k, count):
        e = k // tiles
        t = k - e * tiles
        n = prev_list[1 + e, t]
        own = jnp.maximum(n - tiles, 0)
        tab_ref[1, count] = pack_job(own, t, 0, prev_shift[1 + e, 0, t], prev_shift[1 + e, 1, t])
        return count + (n >= tiles).astype(jnp.int32)

    behind = lax.fori_loop(0, cap, sort, jnp.int32(0), unroll=8)
    pad_jobs(tab_ref, 1, behind, 0, 0, 0)
    tab_ref[0, 0] = behind
    turn_rows(at_ref, a_ref)
    select = selector(4, width)
    cols = (col_a, col_b)
    stream = Stream(prev_hbm, slots, sems, size, OUT_SLOTS, False)
    make_pairs(tab_ref, 1, behind, at_ref, tiles, own_ref, cols, select, "row", boxes, wrap_prev, slots, stream)
    make_pairs(own_tab, 2, own_tab[0, 1], at_ref, 0, own_ref, cols, select, "col", boxes, wrap_next, tensor_ref)
    done = rounded(behind)
    stream.wait(jnp.maximum(done - OUT_SLOTS, 0), done)


def apply_jobs(tab_ref, line, count, at_ref, a_first, cols, select, field_ref, source, stream=None):
    width = field_ref.shape[1]
    size = MATS * width
    tiles = field_ref.shape[0] // 24 - 1

    def columns(j, col_ref):
        for p in range(HALF):
            _, n = target_source(tab_ref[line, HALF * j + p])
            write_columns(col_ref, p, at_ref, a_first + n, select)

    def compute(j, col_ref, _half):
        for p in range(HALF):
            word = tab_ref[line, HALF * j + p]
            t, _ = target_source(word)
            t = t + ((word >> 26) & 1) * tiles
            if stream is None:
                base = pl.multiple_of(((word >> 16) & 255) * size, size)
            else:
                base = stream.base(HALF * j + p)
            acc = [jnp.zeros((8, width), F32)] * 3
            for q in range(width // 8):
                s = [source[pl.ds(base + m * width + 8 * q, 8), :] for m in range(MATS)]
                first = p * width + 8 * q
                mine = [col_ref[first : first + 8, c * width : (c + 1) * width] for c in range(3)]
                lift = s[0] * mine[0] + s[1] * mine[1] + s[2] * mine[2]
                for c in range(3):
                    acc[c] = acc[c] + (s[c] * lift - s[3] * mine[c])
            for c in range(3):
                at = pl.ds(pl.multiple_of((t * 3 + c) * 8, 8), 8)
                field_ref[at, :] = field_ref[at, :] + acc[c]

    if stream is None:
        pipelined(count, columns, compute, cols)
        return
    depth = stream.parts[4]
    total = rounded(count)

    def before(i):
        for p in range(BATCH):
            stream.copy(BATCH * i + p).wait()

    def after(i):
        @pl.when(BATCH * i + depth < total)
        def _():
            for p in range(BATCH):
                stream.copy(BATCH * i + p + depth).start()

    pipelined(count, columns, compute, cols, before, after)


def local_apply_kernel(
    tab_ref, tensor_ref, back_hbm, own_ref, field_ref, a_ref, at_ref, col_a, col_b, slots, sems, *, start
):
    width = own_ref.shape[1]
    tiles = field_ref.shape[0] // 24 - 1
    inner = tab_ref[0, 0]
    stream = Stream(back_hbm, slots, sems, MATS * width, SLOTS, True)
    stream.start(0, jnp.minimum(rounded(inner), SLOTS))
    field_ref[...] = jnp.zeros_like(field_ref)
    a_ref[...] = jnp.zeros_like(a_ref)
    split_rows(a_ref, 0, own_ref, start, tiles, 3)
    turn_rows(at_ref, a_ref)
    select = selector(3, width)
    cols = (col_a, col_b)
    apply_jobs(tab_ref, 1, tiles + inner, at_ref, 0, cols, select, field_ref, tensor_ref)
    apply_jobs(tab_ref, 3, inner, at_ref, 0, cols, select, field_ref, slots, stream)


def cross_apply_kernel(
    par_ref, own_tab, prev_tab, tensor_ref, prev_hbm, own_ref, near_ref, far_ref, inv_ref, part_ref,
    out_ref, field_ref, a_ref, at_ref, col_a, col_b, slots, sems,
    *, start, inv_start,
):
    width = own_ref.shape[1]
    tiles = out_ref.shape[0] // 3
    behind = prev_tab[0, 0]
    stream = Stream(prev_hbm, slots, sems, MATS * width, SLOTS, True)
    stream.start(0, jnp.minimum(rounded(behind), SLOTS))
    par = par_ref[0]
    field_ref[...] = part_ref[...]
    a_ref[...] = jnp.zeros_like(a_ref)
    split_rows(a_ref, par * tiles, near_ref, start, tiles, 3)
    split_rows(a_ref, (1 - par) * tiles, far_ref, start, tiles, 3)
    turn_rows(at_ref, a_ref)
    select = selector(3, width)
    cols = (col_a, col_b)
    apply_jobs(own_tab, 2, own_tab[0, 1], at_ref, 0, cols, select, field_ref, tensor_ref)
    apply_jobs(prev_tab, 1, behind, at_ref, tiles, cols, select, field_ref, slots, stream)
    for t in range(tiles):
        weight = (inv_ref[inv_start + t : inv_start + t + 1, :] - SHIFT) * (1.0 / SCALE)
        for c in range(3):
            at = c * tiles + t
            field = jnp.sum(field_ref[(t * 3 + c) * 8 : (t * 3 + c) * 8 + 8, :], axis=0, keepdims=True)
            mine = own_ref[start + at : start + at + 1, :]
            out_ref[at : at + 1, :] = mine * weight - field * (1.0 / SCALE)


PAIRS = [(i, j) for i in range(ITERS + 1) for j in range(i, ITERS + 1)]


def gram_kernel(*refs, start):
    vectors, out_ref = refs[:-1], refs[-1]
    rows, width = vectors[-1].shape
    lane = lax.broadcasted_iota(jnp.int32, (1, width), 1)
    total = jnp.zeros((1, width), F32)
    starts = (start,) + (0,) * ITERS
    for n, (i, j) in enumerate(PAIRS):
        product = vectors[i][starts[i] : starts[i] + rows, :] * vectors[j][starts[j] : starts[j] + rows, :]
        line = jnp.sum(product, axis=0, keepdims=True)
        total = jnp.where(lane == n, jnp.sum(line, axis=1, keepdims=True), total)
    out_ref[...] = total


def untile_kernel(inv_ref, *refs, start):
    vectors, outs = refs[: ITERS + 1], refs[ITERS + 1 :]
    tiles, width = inv_ref.shape
    starts = (start,) + (0,) * ITERS
    zero = jnp.zeros((8, width), F32)
    for q in range(tiles // 8):
        index = inv_ref[8 * q : 8 * q + 8, :]
        high = index // width
        low = index - high * width

        def step(h, acc):
            hit = high == h
            return tuple(
                jnp.where(hit, lane_pick(spread(vectors[n // 3][pl.ds(starts[n // 3] + n % 3 * tiles + h, 1), :]), low), acc[n])
                for n in range(3 * (ITERS + 1))
            )

        acc = lax.fori_loop(0, tiles, step, (zero,) * (3 * (ITERS + 1)), unroll=8)
        for n in range(3 * (ITERS + 1)):
            for s in range(8):
                at = (8 * q + s) * width
                outs[n // 3][n % 3 : n % 3 + 1, at : at + width] = acc[n][s : s + 1, :]


def output_kernel(parts_ref, *refs):
    vectors, (dip_ref, res_ref) = refs[: ITERS + 1], refs[ITERS + 1 :]
    width = parts_ref.shape[1]
    sums = jnp.sum(parts_ref[...], axis=0, keepdims=True)
    lane = lax.broadcasted_iota(jnp.int32, (1, width), 1)
    gram = {}
    for n, (i, j) in enumerate(PAIRS):
        value = jnp.sum(jnp.where(lane == n, sums, 0.0), axis=1, keepdims=True)
        gram[i, j] = gram[j, i] = jnp.broadcast_to(value, (1, width))

    def add(a, b):
        return b if a is None else a if b is None else a + b

    def inner(a, b):
        total = None
        for i in range(ITERS + 1):
            line = None
            for j in range(ITERS + 1):
                if a[i] is not None and b[j] is not None:
                    line = add(line, b[j] * gram[i, j])
            if line is not None:
                total = add(total, a[i] * line)
        return total

    def operate(a):
        out = [None if v is None else SHIFT * v for v in a]
        for i in range(ITERS):
            if a[i] is not None:
                out[i + 1] = add(out[i + 1], SCALE * a[i])
        return out

    x = [None] * (ITERS + 1)
    r = [jnp.ones((1, width), F32)] + [None] * ITERS
    d = list(r)
    norm = inner(r, r)
    for step in range(ITERS):
        q = operate(d)
        size = norm / inner(d, q)
        x = [add(x[k], None if d[k] is None else size * d[k]) for k in range(ITERS + 1)]
        r = [add(r[k], None if q[k] is None else -size * q[k]) for k in range(ITERS + 1)]
        if step + 1 < ITERS:
            new = inner(r, r)
            ratio = new / norm
            d = [add(r[k], None if d[k] is None else ratio * d[k]) for k in range(ITERS + 1)]
            norm = new
    x = [None if v is None else jnp.broadcast_to(v, (3, width)) for v in x]
    r = [jnp.broadcast_to(v, (3, width)) for v in r]
    for b in range(dip_ref.shape[1] // width):
        at = slice(b * width, (b + 1) * width)
        values = [vectors[k][:, at] for k in range(ITERS + 1)]
        for out, weights in ((dip_ref, x), (res_ref, r)):
            total = None
            for k in range(ITERS + 1):
                if weights[k] is not None:
                    total = add(total, weights[k] * values[k])
            out[:, at] = total


def shape(rows, width, dtype=F32):
    return jax.ShapeDtypeStruct((rows, width), dtype)


def cost(flops):
    return pl.CostEstimate(flops=flops, bytes_accessed=1_000_000, transcendentals=0)


def on_device(positions, polar, field_ext, tile_atom, tile_list, image_shift):
    tiles, links = tile_list.shape
    atoms = tile_atom.shape[0]
    width = atoms // tiles
    slabs = lax.axis_size("gx")
    slab = lax.axis_index("gx")
    rows = 3 * tiles
    cap = tiles * (links - 1)
    size = MATS * width
    boxes = (4.0 * slabs, 128.0, 2.0 * tiles)
    near_pairs = [(i, i ^ 1) for i in range(slabs)]
    far_pairs = [(i, ((i + 1) ^ 1) - 1 if 0 < i < slabs - 1 else slabs - 1 - i) for i in range(slabs)]
    ahead = [(i, (i + 1) % slabs) for i in range(slabs)]

    def swap(value):
        return lax.ppermute(value, "gx", far_pairs), lax.ppermute(value, "gx", near_pairs)

    own_list = tile_list.T
    own_shift = image_shift.transpose(2, 0, 1)
    prev_list = lax.ppermute(own_list, "gx", ahead)
    prev_shift = lax.ppermute(own_shift, "gx", ahead)
    par = jnp.stack([slab % 2, (slab == slabs - 1).astype(jnp.int32), (slab == 0).astype(jnp.int32)])
    par = par.astype(jnp.int32)
    index = tile_atom.reshape(tiles, width)
    packed = pl.pallas_call(
        tile_in_kernel,
        out_shape=shape(8 * tiles, width),
        in_specs=[HBM] * 4,
        out_specs=VMEM,
        scratch_shapes=[
            pltpu.VMEM((3, atoms), F32),
            pltpu.VMEM((1, atoms), F32),
            pltpu.VMEM((3, atoms), F32),
            pltpu.VMEM((tiles, width), jnp.int32),
            pltpu.SemaphoreType.DMA((4,)),
        ],
        compiler_params=params(4),
        name="tile_in",
    )(*(pltpu.with_memory_space_constraint(v, pltpu.MemorySpace.HBM) for v in (positions, polar.reshape(1, -1), field_ext, index)))
    far, near = swap(packed)
    inverse = pl.pallas_call(
        inverse_kernel,
        out_shape=shape(tiles, width, jnp.int32),
        in_specs=[VMEM],
        out_specs=VMEM,
        compiler_params=params(4),
        cost_estimate=cost(4_000_000),
        name="inverse",
    )(index)
    table = shape(4, tiles + cap + PAD, jnp.int32)
    tensor_shape = pltpu.VMEM(((tiles + cap + 1) * size, width), F32)
    stream_shape = pltpu.MemorySpace.HBM(((cap + BATCH) * size, width), F32)

    def scratch(groups, comps, depth):
        col = pltpu.VMEM((HALF * width, comps * width), F32)
        return [
            pltpu.VMEM((groups * tiles * GROUP, width), F32),
            pltpu.VMEM((groups * tiles * width, GROUP), jnp.bfloat16),
            col,
            col,
            pltpu.VMEM((depth * size, width), F32),
            pltpu.SemaphoreType.DMA((depth,)),
        ]

    tensor, back_tensor, own_tab = pl.pallas_call(
        functools.partial(local_pairs_kernel, boxes=boxes),
        out_shape=(tensor_shape, stream_shape, table),
        in_specs=[SMEM, SMEM, VMEM],
        out_specs=(VMEM, HBM, SMEM),
        scratch_shapes=scratch(1, 4, OUT_SLOTS),
        compiler_params=params(12),
        cost_estimate=cost(60_000_000),
        name="local_pairs",
    )(own_list, own_shift, packed)
    tensor, prev_tensor, prev_tab = pl.pallas_call(
        functools.partial(cross_pairs_kernel, boxes=boxes),
        out_shape=(tensor_shape, stream_shape, table),
        in_specs=[SMEM] * 4 + [VMEM] * 4,
        out_specs=(VMEM, HBM, SMEM),
        scratch_shapes=scratch(2, 4, OUT_SLOTS),
        input_output_aliases={7: 0},
        compiler_params=params(12),
        cost_estimate=cost(60_000_000),
        name="cross_pairs",
    )(par, own_tab, prev_list, prev_shift, packed, near, far, tensor)
    prev_tensor = pltpu.with_memory_space_constraint(prev_tensor, pltpu.MemorySpace.HBM)
    back_tensor = pltpu.with_memory_space_constraint(back_tensor, pltpu.MemorySpace.HBM)
    fields = 24 * (tiles + 1)

    def apply(vector, near, far, start):
        part = pl.pallas_call(
            functools.partial(local_apply_kernel, start=start),
            out_shape=shape(fields, width),
            in_specs=[SMEM, VMEM, HBM, VMEM],
            out_specs=VMEM,
            scratch_shapes=scratch(1, 3, SLOTS),
            compiler_params=params(12),
            cost_estimate=cost(60_000_000),
            name="local_apply",
        )(own_tab, tensor, back_tensor, vector)
        return pl.pallas_call(
            functools.partial(cross_apply_kernel, start=start, inv_start=7 * tiles),
            out_shape=shape(rows, width),
            in_specs=[SMEM] * 3 + [VMEM, HBM] + [VMEM] * 5,
            out_specs=VMEM,
            scratch_shapes=[pltpu.VMEM((fields, width), F32)] + scratch(2, 3, SLOTS),
            compiler_params=params(12),
            cost_estimate=cost(60_000_000),
            name="cross_apply",
        )(par, own_tab, prev_tab, tensor, prev_tensor, vector, near, far, packed, part)

    start = 4 * tiles
    basis = [packed]
    vector = apply(packed, near, far, start)
    basis.append(vector)
    for _ in range(ITERS - 1):
        far, near = swap(vector)
        vector = apply(vector, near, far, 0)
        basis.append(vector)
    gram = pl.pallas_call(
        functools.partial(gram_kernel, start=start),
        out_shape=shape(1, width),
        in_specs=[VMEM] * (ITERS + 1),
        out_specs=VMEM,
        compiler_params=params(4),
        name="gram",
    )(*basis)
    parts = lax.all_to_all(jnp.broadcast_to(gram, (slabs, width)), "gx", 0, 0, tiled=True)
    natural = pl.pallas_call(
        functools.partial(untile_kernel, start=start),
        out_shape=(shape(3, atoms),) * (ITERS + 1),
        in_specs=[VMEM] * (ITERS + 2),
        out_specs=(VMEM,) * (ITERS + 1),
        compiler_params=params(4),
        cost_estimate=cost(60_000_000),
        name="untile",
    )(inverse, *basis)
    return pl.pallas_call(
        output_kernel,
        out_shape=(shape(3, atoms), shape(3, atoms)),
        in_specs=[VMEM] * (ITERS + 2),
        out_specs=(VMEM, VMEM),
        compiler_params=params(4),
        name="outputs",
    )(parts, *natural)


def solution(mesh):
    return jax.shard_map(
        on_device,
        mesh=mesh,
        in_specs=(
            P(None, REP_GX),
            P(REP_GX),
            P(None, REP_GX),
            P(REP_GX),
            P(REP_GX, None),
            P(None, REP_GX, None),
        ),
        out_specs=(P(None, REP_GX), P(None, REP_GX)),
        check_vma=False,
    )
```

time: 150 us -> 163 us (1.087)
  Pallas kernels: 96.5 us -> 110 us
    pallas_call x1, Pallas kernels: 9.46 us -> 16.8 us  [on_device(): pl.pallas_call(functools.partial(local_pairs_kernel, boxes=boxes), out_sh...]
    pallas_call x4, Pallas kernels: 27.7 us -> 34.1 us  [apply(): pl.pallas_call(functools.partial(local_apply_kernel, start=start), out_sh...]
    pallas_call x4, Pallas kernels: 38.7 us -> 35.2 us  [apply(): pl.pallas_call(functools.partial(cross_apply_kernel, start=start, inv_sta...]
    all_to_all x1, starting transfers between devices: 9.07 us -> 12.2 us  [on_device(): lax.all_to_all(jnp.broadcast_to(gram, (slabs, width)), 'gx', 0, 0, tiled=...]
    pallas_call x1, Pallas kernels: 13 us -> 15.8 us  [on_device(): pl.pallas_call(functools.partial(cross_pairs_kernel, boxes=boxes), out_sh...]
    ppermute x4, starting transfers between devices: 2.16 us -> 0.01 us  [swap(): lax.ppermute(value, 'gx', far_pairs)]
  transfers between devices with their start and end apart: 11 -> 11, of which waited for: 1 -> 1; matrix products, arithmetic and copies ran while one was open for 0% -> 0% of each run, Pallas kernels for 23% -> 29%
where the time goes in v3:
time: 163 us
  Pallas kernels  110 us (67%)
  starting transfers between devices  42.1 us (26%)
  waiting for transfers between devices  8.18 us (5%)
  local copies, waits for them, and re-layouts  2.04 us (1%)
    pallas_call x4, Pallas kernels, apply(): pl.pallas_call(functools.partial(cross_apply_kernel, start=start, inv_sta...  35.2 us
    pallas_call x4, Pallas kernels, apply(): pl.pallas_call(functools.partial(local_apply_kernel, start=start), out_sh...  34.1 us
    ppermute x4, starting transfers between devices, swap(): lax.ppermute(value, 'gx', near_pairs)  28.1 us
    pallas_call x1, Pallas kernels, on_device(): pl.pallas_call(functools.partial(local_pairs_kernel, boxes=boxes), out_sh...  16.8 us
    pallas_call x1, Pallas kernels, on_device(): pl.pallas_call(functools.partial(cross_pairs_kernel, boxes=boxes), out_sh...  15.8 us
    all_to_all x1, starting transfers between devices, on_device(): lax.all_to_all(jnp.broadcast_to(gram, (slabs, width)), 'gx', 0, 0, tiled=...  12.2 us
    all_to_all x1, waiting for transfers between devices, on_device(): lax.all_to_all(jnp.broadcast_to(gram, (slabs, width)), 'gx', 0, 0, tiled=...  8.16 us
  transfers between devices with their start and end apart: 11, of which 1 were waited for; matrix products, arithmetic and copies ran while one was open for 0% of the time, Pallas kernels for 29%

profile of v3, /device:TPU:513, one launch (start us, length us, event | category | flops | bytes accessed | tf_op | source)
XLA Modules:
  0.0 162.8 jit_solution(15938362471979646830)
XLA Ops:
  0.6 2.5 %tile_in.1.own_ref.inv_ref.refs_0_ = f32[256,128]{1,0:T(8,128)S(1)} custom-call(f32[3,4096]{1,0:T(4,128)} %pos_hbm.1, f32[1,4096]{1,0:T(1,128)} %bitcast.17, f32[3,4096]{1,0:T(4,128)} %fld_hbm.1, s32[32,128]{1,0:T(8,128)} %bitcast.10), custom_call_target="tpu_custom_call" | custom-call | tf_op jit(solution)/shard_map/tile_in/pallas_call | solution.py:615
  3.1 20.5 %collective-permute-start.2 = (f32[256,128]{1,0:T(8,128)S(1)}, f32[256,128]{1,0:T(8,128)S(1)}, u32[]{:S(2)}, u32[]{:S(2)}) collective-permute-start(f32[256,128]{1,0:T(8,128)S(1)} %tile_in.1.own_ref.inv_ref.refs_0_), channel_id=1, source_target_pairs={{0,1},{1,0},{2,3},{3,2},{4,5},{5,4},{6,7},{7,6},{8,9},{9,8},{10,11... | collective-permute-start | bytes 393224 | tf_op jit(solution)/shard_map/ppermute | solution.py:606
  23.6 0.0 collective-permute-start.3
  23.6 1.7 %collective-permute-start.1 = (s32[3,2,32]{2,1,0:T(2,128)}, s32[3,2,32]{2,1,0:T(2,128)S(1)}, u32[]{:S(2)}, u32[]{:S(2)}) collective-permute-start(s32[3,2,32]{2,1,0:T(2,128)} %bitcast.13), channel_id=1, source_target_pairs={{0,1},{1,2},{2,3},{3,4},{4,5},{5,6},{6,7},{7,8},{8,9},{9,10},{10,1... | collective-permute-start | bytes 2312 | tf_op jit(solution)/shard_map/ppermute | solution.py:611
  25.4 0.0 collective-permute-start
  25.4 0.1 pad_add_fusion.par_ref
  25.5 0.0 copy-start.1
  25.5 0.7 copy-done.1
  26.2 0.0 copy-start.2
  26.2 0.7 copy-done.2
  26.9 16.8 %local_pairs.1 = (f32[49664,128]{1,0:T(8,128)S(1)}, f32[36864,128]{1,0:T(8,128)}, s32[4,108]{1,0:T(4,128)S(1)}) custom-call(s32[3,32]{1,0:T(4,128)S(1)} %bitcast.16, s32[3,2,32]{2,1,0:T(2,128)S(1)} %bitcast.14, f32[256,128]{1,0:T(8,128)S(1)} %tile_in.1.own_ref.inv_ref.refs_0_), custom_call_target="tpu_custom_call" | custom-call | flops 60000000 | bytes 1000000 | tf_op jit(solution)/shard_map/local_pairs/pallas_call | solution.py:655
  43.6 0.0 collective-permute-done.prev_list
  43.6 0.0 collective-permute-done.1.prev_shift
  43.7 0.0 collective-permute-done.2.near_ref
  43.7 0.0 collective-permute-done.3.far_ref
  43.7 15.8 %cross_pairs.1 = (f32[49664,128]{1,0:T(8,128)S(1)}, f32[36864,128]{1,0:T(8,128)}, s32[4,108]{1,0:T(4,128)S(1)}) custom-call(s32[3]{0:T(128)S(1)} %pad_add_fusion.par_ref, s32[4,108]{1,0:T(4,128)S(1)} %get-tuple-element.13.own_tab.tab_ref, s32[3,32]{1,0:T(4,128)S(1)} %collective-permute-done.prev_list, ...), custom_call_target="tpu_custom_call", output_to_operand_aliasing={{0}: (7, {})} | custom-call | flops 60000000 | bytes 1000000 | tf_op jit(solution)/shard_map/cross_pairs/pallas_call | solution.py:665
  59.5 8.5 %local_apply.4.part_ref = f32[792,128]{1,0:T(8,128)S(1)} custom-call(s32[4,108]{1,0:T(4,128)S(1)} %get-tuple-element.13.own_tab.tab_ref, f32[49664,128]{1,0:T(8,128)S(1)} %get-tuple-element.16.tensor_ref, f32[36864,128]{1,0:T(8,128)} %get-tuple-element.18.back_hbm, f32[256,128]{1,0:T(8,128)S(1)} %tile_in.1.own_ref.inv_ref.refs_0_), custom_call_target="tpu_custom_call" | custom-call | flops 60000000 | bytes 1000000 | tf_op jit(solution)/shard_map/local_apply/pallas_call | solution.py:681
  68.1 8.9 %cross_apply.4.own_ref.refs_1_ = f32[96,128]{1,0:T(8,128)S(1)} custom-call(s32[3]{0:T(128)S(1)} %pad_add_fusion.par_ref, s32[4,108]{1,0:T(4,128)S(1)} %get-tuple-element.13.own_tab.tab_ref, s32[4,108]{1,0:T(4,128)S(1)} %get-tuple-element.15.prev_tab, f32[49664,128]{1,0:T(8,128)S(1)} %get-tuple-element.16.tensor_ref, ...), custom_call_target="tpu_custom_call" | custom-call | flops 60000000 | bytes 1000000 | tf_op jit(solution)/shard_map/cross_apply/pallas_call | solution.py:691
  76.9 0.6 collective-permute-start.4
  77.6 0.0 collective-permute-start.5
  77.6 8.5 %local_apply.5.part_ref = f32[792,128]{1,0:T(8,128)S(1)} custom-call(s32[4,108]{1,0:T(4,128)S(1)} %get-tuple-element.13.own_tab.tab_ref, f32[49664,128]{1,0:T(8,128)S(1)} %get-tuple-element.16.tensor_ref, f32[36864,128]{1,0:T(8,128)} %get-tuple-element.18.back_hbm, f32[96,128]{1,0:T(8,128)S(1)} %cross_apply.4.own_ref.refs_1_), custom_call_target="tpu_custom_call" | custom-call | flops 60000000 | bytes 1000000 | tf_op jit(solution)/shard_map/local_apply/pallas_call | solution.py:681
  86.1 0.0 collective-permute-done.4.near_ref
  86.1 0.0 collective-permute-done.5.far_ref
  86.1 8.7 %cross_apply.5.own_ref.refs_2_ = f32[96,128]{1,0:T(8,128)S(1)} custom-call(s32[3]{0:T(128)S(1)} %pad_add_fusion.par_ref, s32[4,108]{1,0:T(4,128)S(1)} %get-tuple-element.13.own_tab.tab_ref, s32[4,108]{1,0:T(4,128)S(1)} %get-tuple-element.15.prev_tab, f32[49664,128]{1,0:T(8,128)S(1)} %get-tuple-element.16.tensor_ref, ...), custom_call_target="tpu_custom_call" | custom-call | flops 60000000 | bytes 1000000 | tf_op jit(solution)/shard_map/cross_apply/pallas_call | solution.py:691
  94.8 6.0 %collective-permute-start.6 = (f32[96,128]{1,0:T(8,128)S(1)}, f32[96,128]{1,0:T(8,128)S(1)}, u32[]{:S(2)}, u32[]{:S(2)}) collective-permute-start(f32[96,128]{1,0:T(8,128)S(1)} %cross_apply.5.own_ref.refs_2_), channel_id=1, source_target_pairs={{0,1},{1,0},{2,3},{3,2},{4,5},{5,4},{6,7},{7,6},{8,9},{9,8},{10,11... | collective-permute-start | bytes 147464 | tf_op jit(solution)/shard_map/ppermute | solution.py:606
  100.8 0.0 collective-permute-start.7
  100.8 8.5 %local_apply.6.part_ref = f32[792,128]{1,0:T(8,128)S(1)} custom-call(s32[4,108]{1,0:T(4,128)S(1)} %get-tuple-element.13.own_tab.tab_ref, f32[49664,128]{1,0:T(8,128)S(1)} %get-tuple-element.16.tensor_ref, f32[36864,128]{1,0:T(8,128)} %get-tuple-element.18.back_hbm, f32[96,128]{1,0:T(8,128)S(1)} %cross_apply.5.own_ref.refs_2_), custom_call_target="tpu_custom_call" | custom-call | flops 60000000 | bytes 1000000 | tf_op jit(solution)/shard_map/local_apply/pallas_call | solution.py:681
  109.4 0.0 collective-permute-done.6.near_ref
  109.4 0.0 collective-permute-done.7.far_ref
  109.4 8.7 %cross_apply.6.own_ref.refs_3_ = f32[96,128]{1,0:T(8,128)S(1)} custom-call(s32[3]{0:T(128)S(1)} %pad_add_fusion.par_ref, s32[4,108]{1,0:T(4,128)S(1)} %get-tuple-element.13.own_tab.tab_ref, s32[4,108]{1,0:T(4,128)S(1)} %get-tuple-element.15.prev_tab, f32[49664,128]{1,0:T(8,128)S(1)} %get-tuple-element.16.tensor_ref, ...), custom_call_target="tpu_custom_call" | custom-call | flops 60000000 | bytes 1000000 | tf_op jit(solution)/shard_map/cross_apply/pallas_call | solution.py:691
  118.1 1.0 collective-permute-start.8
  119.1 0.0 collective-permute-start.9
  119.1 8.5 %local_apply.7.part_ref = f32[792,128]{1,0:T(8,128)S(1)} custom-call(s32[4,108]{1,0:T(4,128)S(1)} %get-tuple-element.13.own_tab.tab_ref, f32[49664,128]{1,0:T(8,128)S(1)} %get-tuple-element.16.tensor_ref, f32[36864,128]{1,0:T(8,128)} %get-tuple-element.18.back_hbm, f32[96,128]{1,0:T(8,128)S(1)} %cross_apply.6.own_ref.refs_3_), custom_call_target="tpu_custom_call" | custom-call | flops 60000000 | bytes 1000000 | tf_op jit(solution)/shard_map/local_apply/pallas_call | solution.py:681
  127.6 0.0 copy-start
  127.6 0.0 collective-permute-done.8.near_ref
  127.7 0.0 collective-permute-done.9.far_ref
  127.7 8.9 %cross_apply.7.refs_4_ = f32[96,128]{1,0:T(8,128)S(1)} custom-call(s32[3]{0:T(128)S(1)} %pad_add_fusion.par_ref, s32[4,108]{1,0:T(4,128)S(1)} %get-tuple-element.13.own_tab.tab_ref, s32[4,108]{1,0:T(4,128)S(1)} %get-tuple-element.15.prev_tab, f32[49664,128]{1,0:T(8,128)S(1)} %get-tuple-element.16.tensor_ref, f32[36864,128]{1,0:T(8,128)} %get-tuple-element.17.prev_hbm, ...), custom_call_target="tpu_custom_call" | custom-call | flops 60000000 | bytes 1000000 | tf_op jit(solution)/shard_map/cross_apply/pallas_call | solution.py:691
  136.6 0.1 gram.1
  136.7 0.7 broadcast_in_dim.2
  137.4 12.2 %all-to-all-start = ((f32[128,1,128]{2,1,0:T(1,128)}), f32[128,1,128]{2,1,0:T(1,128)S(1)}, u32[]{:S(2)}, u32[]{:S(2)}) async-start(f32[128,1,128]{2,1,0:T(1,128)} %broadcast_in_dim.2), calls=%async_computation | async-start | bytes 131072 | tf_op jit(solution)/shard_map/all_to_all | solution.py:718
  149.6 0.0 copy-done
  149.6 0.8 inverse.1.inv_ref
  150.4 3.2 %untile.1 = (f32[3,4096]{1,0:T(4,128)S(1)}, f32[3,4096]{1,0:T(4,128)S(1)}, f32[3,4096]{1,0:T(4,128)S(1)}, f32[3,4096]{1,0:T(4,128)S(1)}, f32[3,4096]{1,0:T(4,128)S(1)}) custom-call(s32[32,128]{1,0:T(8,128)S(1)} %inverse.1.inv_ref, f32[256,128]{1,0:T(8,128)S(1)} %tile_in.1.own_ref.inv_ref.refs_0_, f32[96,128]{1,0:T(8,128)S(1)} %cross_apply.4.own_ref.refs_1_, ...), custom_call_target="tpu_custom_call" | custom-call | flops 60000000 | bytes 1000000 | tf_op jit(solution)/shard_map/untile/pallas_call | solution.py:719
  153.7 8.2 %all-to-all-done = f32[128,1,128]{2,1,0:T(1,128)S(1)} async-done(((f32[128,1,128]{2,1,0:T(1,128)}), f32[128,1,128]{2,1,0:T(1,128)S(1)}, u32[]{:S(2)}, u32[]{:S(2)}) %all-to-all-start) | async-done | bytes 65568 | tf_op jit(solution)/shard_map/all_to_all | solution.py:718
  161.9 0.9 outputs.1
Async XLA Ops:
  3.1 40.6 %collective-permute-start.2 = (f32[256,128]{1,0:T(8,128)S(1)}, f32[256,128]{1,0:T(8,128)S(1)}, u32[]{:S(2)}, u32[]{:S(2)}) collective-permute-start(f32[256,128]{1,0:T(8,128)S(1)} %tile_in.1.own_ref.inv_ref.refs_0_), channel_id=1, source_target_pairs={{0,1},{1,0},{2,3},{3,2},{4,5},{5,4},{6,7},{7,6},{8,9},{9,8},{10,11... | collective-permute-start | bytes 393224 | tf_op jit(solution)/shard_map/ppermute | solution.py:606
  23.6 20.0 %collective-permute-start.3 = (f32[256,128]{1,0:T(8,128)S(1)}, f32[256,128]{1,0:T(8,128)S(1)}, u32[]{:S(2)}, u32[]{:S(2)}) collective-permute-start(f32[256,128]{1,0:T(8,128)S(1)} %tile_in.1.own_ref.inv_ref.refs_0_), channel_id=1, source_target_pairs={{0,127},{1,2},{2,1},{3,4},{4,3},{5,6},{6,5},{7,8},{8,7},{9,10},{10... | collective-permute-start | bytes 393224 | tf_op jit(solution)/shard_map/ppermute | solution.py:606
  23.6 20.0 %collective-permute-start.1 = (s32[3,2,32]{2,1,0:T(2,128)}, s32[3,2,32]{2,1,0:T(2,128)S(1)}, u32[]{:S(2)}, u32[]{:S(2)}) collective-permute-start(s32[3,2,32]{2,1,0:T(2,128)} %bitcast.13), channel_id=1, source_target_pairs={{0,1},{1,2},{2,3},{3,4},{4,5},{5,6},{6,7},{7,8},{8,9},{9,10},{10,1... | collective-permute-start | bytes 2312 | tf_op jit(solution)/shard_map/ppermute | solution.py:611
  25.4 18.2 %collective-permute-start = (s32[3,32]{1,0:T(4,128)}, s32[3,32]{1,0:T(4,128)S(1)}, u32[]{:S(2)}, u32[]{:S(2)}) collective-permute-start(s32[3,32]{1,0:T(4,128)} %bitcast.15), channel_id=1, source_target_pairs={{0,1},{1,2},{2,3},{3,4},{4,5},{5,6},{6,7},{7,8},{8,9},{9,10},{10,1... | collective-permute-start | bytes 1160 | tf_op jit(solution)/shard_map/ppermute | solution.py:610
  25.5 0.7 copy-start.1
  26.2 0.7 copy-start.2
  76.9 9.2 %collective-permute-start.4 = (f32[96,128]{1,0:T(8,128)S(1)}, f32[96,128]{1,0:T(8,128)S(1)}, u32[]{:S(2)}, u32[]{:S(2)}) collective-permute-start(f32[96,128]{1,0:T(8,128)S(1)} %cross_apply.4.own_ref.refs_1_), channel_id=1, source_target_pairs={{0,1},{1,0},{2,3},{3,2},{4,5},{5,4},{6,7},{7,6},{8,9},{9,8},{10,11... | collective-permute-start | bytes 147464 | tf_op jit(solution)/shard_map/ppermute | solution.py:606
  77.6 8.6 %collective-permute-start.5 = (f32[96,128]{1,0:T(8,128)S(1)}, f32[96,128]{1,0:T(8,128)S(1)}, u32[]{:S(2)}, u32[]{:S(2)}) collective-permute-start(f32[96,128]{1,0:T(8,128)S(1)} %cross_apply.4.own_ref.refs_1_), channel_id=1, source_target_pairs={{0,127},{1,2},{2,1},{3,4},{4,3},{5,6},{6,5},{7,8},{8,7},{9,10},{10... | collective-permute-start | bytes 147464 | tf_op jit(solution)/shard_map/ppermute | solution.py:606
  94.8 14.6 %collective-permute-start.6 = (f32[96,128]{1,0:T(8,128)S(1)}, f32[96,128]{1,0:T(8,128)S(1)}, u32[]{:S(2)}, u32[]{:S(2)}) collective-permute-start(f32[96,128]{1,0:T(8,128)S(1)} %cross_apply.5.own_ref.refs_2_), channel_id=1, source_target_pairs={{0,1},{1,0},{2,3},{3,2},{4,5},{5,4},{6,7},{7,6},{8,9},{9,8},{10,11... | collective-permute-start | bytes 147464 | tf_op jit(solution)/shard_map/ppermute | solution.py:606
  100.8 8.6 %collective-permute-start.7 = (f32[96,128]{1,0:T(8,128)S(1)}, f32[96,128]{1,0:T(8,128)S(1)}, u32[]{:S(2)}, u32[]{:S(2)}) collective-permute-start(f32[96,128]{1,0:T(8,128)S(1)} %cross_apply.5.own_ref.refs_2_), channel_id=1, source_target_pairs={{0,127},{1,2},{2,1},{3,4},{4,3},{5,6},{6,5},{7,8},{8,7},{9,10},{10... | collective-permute-start | bytes 147464 | tf_op jit(solution)/shard_map/ppermute | solution.py:606
  118.1 9.5 %collective-permute-start.8 = (f32[96,128]{1,0:T(8,128)S(1)}, f32[96,128]{1,0:T(8,128)S(1)}, u32[]{:S(2)}, u32[]{:S(2)}) collective-permute-start(f32[96,128]{1,0:T(8,128)S(1)} %cross_apply.6.own_ref.refs_3_), channel_id=1, source_target_pairs={{0,1},{1,0},{2,3},{3,2},{4,5},{5,4},{6,7},{7,6},{8,9},{9,8},{10,11... | collective-permute-start | bytes 147464 | tf_op jit(solution)/shard_map/ppermute | solution.py:606
  119.1 8.6 %collective-permute-start.9 = (f32[96,128]{1,0:T(8,128)S(1)}, f32[96,128]{1,0:T(8,128)S(1)}, u32[]{:S(2)}, u32[]{:S(2)}) collective-permute-start(f32[96,128]{1,0:T(8,128)S(1)} %cross_apply.6.own_ref.refs_3_), channel_id=1, source_target_pairs={{0,127},{1,2},{2,1},{3,4},{4,3},{5,6},{6,5},{7,8},{8,7},{9,10},{10... | collective-permute-start | bytes 147464 | tf_op jit(solution)/shard_map/ppermute | solution.py:606
  127.6 22.0 %copy-start = (s32[4096]{0:T(1024)S(1)}, s32[4096]{0:T(1024)}, u32[]{:S(2)}) copy-start(s32[4096]{0:T(1024)} %param.9) | copy-start | bytes 49156
  137.4 24.4 %all-to-all-start = ((f32[128,1,128]{2,1,0:T(1,128)}), f32[128,1,128]{2,1,0:T(1,128)S(1)}, u32[]{:S(2)}, u32[]{:S(2)}) async-start(f32[128,1,128]{2,1,0:T(1,128)} %broadcast_in_dim.2), calls=%async_computation | async-start | bytes 131072 | tf_op jit(solution)/shard_map/all_to_all | solution.py:718
